TPU v7x, 32 devices: a whole 2x2x4 slice. The times are simulated.
32 devices in a mesh: shard: 4 (over y, x), ctx: 2 (over core), tp: 4 (over z).
Axes of the slice: x: 2, y: 2, z: 4, core: 2. Of those that a mesh axis runs over, the one named last changes fastest.
Arguments:
- hidden_in: bfloat16 [4, 4, 512, 2048], P('shard', 'ctx'), may hold values from -6 to 6
- grad_out: bfloat16 [4, 4, 512, 2048], P('shard', 'ctx'), may hold values from -6 to 6
- segment_ids: int32 [4, 2048], P('shard'), may hold values from 0 to 5, never falling along the last dimension, each value on 1 to 1024 neighbouring positions
- group_order: int32 [4], replicated, may hold values from 0 to 3, each once
- ln1_gain: bfloat16 [2048], P('shard'), may hold values from 0.5 to 1.5
- ln1_bias: bfloat16 [2048], P('shard'), may hold values from -3 to 3
- qkv_weight: bfloat16 [2048, 6144], P('shard', 'tp'), may hold values from -3 to 3
- qkv_bias: bfloat16 [4, 1536], P('tp', 'shard'), may hold values from -3 to 3
- dense_weight: bfloat16 [2048, 2048], P('shard', 'tp'), may hold values from -0.375 to 0.375
- dense_bias: bfloat16 [2048], P('shard'), may hold values from -3 to 3
- ln2_gain: bfloat16 [2048], P('shard'), may hold values from 0.5 to 1.5
- ln2_bias: bfloat16 [2048], P('shard'), may hold values from -3 to 3
- up_weight: bfloat16 [2048, 8192], P('shard', 'tp'), may hold values from -0.125 to 0.125
- up_bias: bfloat16 [4, 2048], P('tp', 'shard'), may hold values from -3 to 3
- down_weight: bfloat16 [2048, 8192], P('shard', 'tp'), may hold values from -0.0625 to 0.0625
- down_bias: bfloat16 [2048], P('shard'), may hold values from -3 to 3
Outputs:
- output: float32 [4, 4, 512, 2048], P('shard', 'ctx', None, 'tp')
- input_grad: float32 [4, 4, 512, 2048], P('shard', 'ctx', None, 'tp')
- ln1_gain_grad: float32 [2048], P('shard')
- ln1_bias_grad: float32 [2048], P('shard')
- qkv_weight_grad: float32 [2048, 6144], P('shard', 'tp')
- qkv_bias_grad: float32 [4, 1536], P('tp', 'shard')
- dense_weight_grad: float32 [2048, 2048], P('shard', 'tp')
- out_bias_grad: float32 [2048], P('shard')
- ln2_gain_grad: float32 [2048], P('shard')
- ln2_bias_grad: float32 [2048], P('shard')
- up_weight_grad: float32 [2048, 8192], P('shard', 'tp')
- up_bias_grad: float32 [4, 2048], P('tp', 'shard')
- down_weight_grad: float32 [2048, 8192], P('shard', 'tp')
Inputs may be any that keep to these rules, and one draw needn't show every extreme that they name: A permutation: stored block k of every row holds the row's places group_order[k] * 512 to group_order[k] * 512 + 511. `segment_ids`: never falling along a row; each segment has 1 to 1024 tokens, one exactly 1024.
All inputs are finite; a program needn't handle non-finite values.
Results may differ from a plain program's by a relative error of at most 0.012.
Values may be sent and summed in bfloat16 or wider, within the bound.
A program may use at most 320 MiB of HBM per device.

v0:
```python
import math

import jax
import jax.numpy as jnp
from jax import lax
from jax.sharding import PartitionSpec as P

HD = 256
ROT = 64


EPSILON = 1e-05
ROTARY_BASE = 10000.0


def layer_norm(values, gain_vec, shift_vec):
    mean_row = jnp.mean(values, axis=-1, keepdims=True)
    centered = values - mean_row
    inverse = lax.rsqrt(jnp.mean(centered * centered, axis=-1, keepdims=True) + EPSILON)
    normed = centered * inverse
    return (normed * gain_vec + shift_vec, normed, inverse)


def norm_backward(grad_norm, normed, inverse, gain_vec):
    scaled = grad_norm * gain_vec
    inner_term = (
        scaled
        - jnp.mean(scaled, axis=-1, keepdims=True)
        - normed * jnp.mean(scaled * normed, axis=-1, keepdims=True)
    )
    return (inverse * inner_term, jnp.sum(grad_norm * normed, axis=0), jnp.sum(grad_norm, axis=0))


def segment_positions(segments):
    length_all = segments.shape[1]
    index_row = jnp.arange(length_all, dtype=jnp.int32)[None, :]
    changed = jnp.concatenate(
        [jnp.ones((segments.shape[0], 1), dtype=jnp.bool_), segments[:, 1:] != segments[:, :-1]],
        axis=1,
    )
    seg_start = jnp.where(changed, index_row, jnp.zeros_like(segments))
    seg_first = lax.cummax(seg_start, axis=1)
    return index_row - seg_first


def rotary_tables(positions):
    half_rot = ROT // 2
    frequency = ROTARY_BASE ** (-2.0 * jnp.arange(half_rot, dtype=jnp.float32) / ROT)
    angles = positions.astype(jnp.float32)[:, None] * frequency[None, :]
    cosine_table = jnp.concatenate([jnp.cos(angles), jnp.cos(angles)], axis=-1)
    sine_table = jnp.concatenate([jnp.sin(angles), jnp.sin(angles)], axis=-1)
    return (cosine_table, sine_table)


def rotate(values, cosine_table, sine_table):
    half_rot = ROT // 2
    rot_part = values[..., :ROT]
    turned = jnp.concatenate([-rot_part[..., half_rot:], rot_part[..., :half_rot]], axis=-1)
    rotated = rot_part * cosine_table[:, None, :] + turned * sine_table[:, None, :]
    return jnp.concatenate([rotated, values[..., ROT:]], axis=-1)


def rotate_back(grad_values, cosine_table, sine_table):
    half_rot = ROT // 2
    rot_part = grad_values[..., :ROT]
    moved_part = rot_part * sine_table[:, None, :]
    turned = jnp.concatenate([-moved_part[..., half_rot:], moved_part[..., :half_rot]], axis=-1)
    return jnp.concatenate(
        [rot_part * cosine_table[:, None, :] - turned, grad_values[..., ROT:]], axis=-1
    )


def gelu_slope(pre_act):
    cdf_part = 0.5 * (1.0 + jax.scipy.special.erf(pre_act / math.sqrt(2.0)))
    return cdf_part + pre_act * jnp.exp(-0.5 * pre_act * pre_act) / math.sqrt(2.0 * math.pi)


def contract_first(left_mat, right_mat):
    return lax.dot_general(
        left_mat, right_mat, (((0,), (0,)), ((), ())), preferred_element_type=jnp.float32
    )


def contract_last(left_mat, right_mat):
    return lax.dot_general(
        left_mat, right_mat, (((1,), (1,)), ((), ())), preferred_element_type=jnp.float32
    )


def local(
    hidden_in,
    grad_out,
    segment_ids,
    group_order,
    ln1_gain,
    ln1_bias,
    qkv_weight,
    qkv_bias,
    dense_weight,
    dense_bias,
    ln2_gain,
    ln2_bias,
    up_weight,
    up_bias,
    down_weight,
    down_bias,
):
    rows_dev, groups_dev, block_len, full_width = hidden_in.shape
    tokens = rows_dev * groups_dev * block_len
    row_tokens = groups_dev * block_len
    seq_len = segment_ids.shape[1]
    tp_count = lax.axis_size("tp")
    tp_rank = lax.axis_index("tp")
    ctx_rank = lax.axis_index("ctx")
    slice_width = full_width // tp_count
    score_scale = 1.0 / math.sqrt(HD)
    gain_one, shift_one, w_qkv, bias_qkv, w_dense, bias_dense = (
        lax.all_gather(ln1_gain, "shard", axis=0, tiled=True),
        lax.all_gather(ln1_bias, "shard", axis=0, tiled=True),
        lax.all_gather(qkv_weight, "shard", axis=0, tiled=True),
        lax.all_gather(qkv_bias, "shard", axis=1, tiled=True),
        lax.all_gather(dense_weight, "shard", axis=0, tiled=True),
        lax.all_gather(dense_bias, "shard", axis=0, tiled=True),
    )
    gain_two, shift_two, w_up, bias_up, w_down, bias_down = (
        lax.all_gather(ln2_gain, "shard", axis=0, tiled=True),
        lax.all_gather(ln2_bias, "shard", axis=0, tiled=True),
        lax.all_gather(up_weight, "shard", axis=0, tiled=True),
        lax.all_gather(up_bias, "shard", axis=1, tiled=True),
        lax.all_gather(down_weight, "shard", axis=0, tiled=True),
        lax.all_gather(down_bias, "shard", axis=0, tiled=True),
    )
    heads_dev = w_qkv.shape[1] // (3 * HD)
    offsets = jnp.arange(block_len, dtype=jnp.int32)
    place_all = (group_order[:, None] * block_len + offsets[None, :]).reshape(seq_len)
    place_mine = lax.dynamic_slice_in_dim(place_all, ctx_rank * row_tokens, row_tokens)
    positions = segment_positions(segment_ids)
    seg_keys = segment_ids[:, place_all]
    seg_query = segment_ids[:, place_mine]
    cosine_table, sine_table = rotary_tables(positions[:, place_mine].reshape(tokens))
    causal_ok = place_all[None, :] <= place_mine[:, None]
    x_float = hidden_in.reshape(tokens, full_width).astype(jnp.float32)
    normed_one, hat_one, inv_one = layer_norm(
        x_float, gain_one.astype(jnp.float32), shift_one.astype(jnp.float32)
    )
    acts_one = normed_one.astype(jnp.bfloat16)
    projected = (
        jnp.dot(acts_one, w_qkv, preferred_element_type=jnp.float32)
        + bias_qkv.reshape(-1).astype(jnp.float32)
    ).reshape(tokens, heads_dev, 3, HD)
    query_b = rotate(projected[:, :, 0], cosine_table, sine_table).astype(jnp.bfloat16)
    key_b = rotate(projected[:, :, 1], cosine_table, sine_table).astype(jnp.bfloat16)
    value_b = projected[:, :, 2].astype(jnp.bfloat16)
    kv_shape = (rows_dev, groups_dev, block_len, heads_dev, HD)
    key_all, value_all = (
        lax.all_gather(key_b.reshape(kv_shape), "ctx", axis=1, tiled=True),
        lax.all_gather(value_b.reshape(kv_shape), "ctx", axis=1, tiled=True),
    )
    query_rows = query_b.reshape(rows_dev, row_tokens, heads_dev, HD)

    def row_scores(query_row, key_row, row_index):
        scores = (
            jnp.einsum("qhd,khd->hqk", query_row, key_row, preferred_element_type=jnp.float32)
            * score_scale
        )
        allowed = causal_ok & (seg_query[row_index][:, None] == seg_keys[row_index][None, :])
        return jnp.where(allowed[None], scores, -jnp.inf)

    row_index = 0
    key_row = key_all[row_index].reshape(seq_len, heads_dev, HD)
    value_row = value_all[row_index].reshape(seq_len, heads_dev, HD)
    scores = row_scores(query_rows[row_index], key_row, row_index)
    top_score = jnp.max(scores, axis=-1, keepdims=True)
    log_total = top_score + jnp.log(jnp.sum(jnp.exp(scores - top_score), axis=-1, keepdims=True))
    prob_b = jnp.exp(scores - log_total).astype(jnp.bfloat16)
    attn_rows = [
        jnp.einsum("hqk,khd->qhd", prob_b, value_row, preferred_element_type=jnp.float32).astype(
            jnp.bfloat16
        )
    ]
    total_rows = [log_total]
    attn_heads = jnp.stack(attn_rows, axis=0)
    attn_out = attn_heads.reshape(tokens, heads_dev * HD)
    attn_part = contract_last(attn_out, w_dense)
    normed_two, hat_two, inv_two = layer_norm(
        x_float, gain_two.astype(jnp.float32), shift_two.astype(jnp.float32)
    )
    acts_two = normed_two.astype(jnp.bfloat16)
    pre_act = jnp.dot(acts_two, w_up, preferred_element_type=jnp.float32) + bias_up.reshape(
        -1
    ).astype(jnp.float32)
    hidden_b = jax.nn.gelu(pre_act, approximate=False).astype(jnp.bfloat16)
    mlp_part = contract_last(hidden_b, w_down)
    partial_out = (attn_part + mlp_part).reshape(rows_dev, groups_dev, block_len, full_width)
    summed_out = lax.psum_scatter(partial_out, "tp", scatter_dimension=3, tiled=True)
    out_shift = bias_dense.astype(jnp.float32) + bias_down.astype(jnp.float32)
    shift_slice = lax.dynamic_slice_in_dim(out_shift, tp_rank * slice_width, slice_width)
    x_slice = lax.dynamic_slice_in_dim(hidden_in, tp_rank * slice_width, slice_width, 3).astype(
        jnp.float32
    )
    output = x_slice + summed_out + shift_slice
    gain_one, shift_one, w_qkv, bias_qkv, w_dense, bias_dense = (
        lax.all_gather(ln1_gain, "shard", axis=0, tiled=True),
        lax.all_gather(ln1_bias, "shard", axis=0, tiled=True),
        lax.all_gather(qkv_weight, "shard", axis=0, tiled=True),
        lax.all_gather(qkv_bias, "shard", axis=1, tiled=True),
        lax.all_gather(dense_weight, "shard", axis=0, tiled=True),
        lax.all_gather(dense_bias, "shard", axis=0, tiled=True),
    )
    gain_two, shift_two, w_up, bias_up, w_down, bias_down = (
        lax.all_gather(ln2_gain, "shard", axis=0, tiled=True),
        lax.all_gather(ln2_bias, "shard", axis=0, tiled=True),
        lax.all_gather(up_weight, "shard", axis=0, tiled=True),
        lax.all_gather(up_bias, "shard", axis=1, tiled=True),
        lax.all_gather(down_weight, "shard", axis=0, tiled=True),
        lax.all_gather(down_bias, "shard", axis=0, tiled=True),
    )
    key_all, value_all = (
        lax.all_gather(key_b.reshape(kv_shape), "ctx", axis=1, tiled=True),
        lax.all_gather(value_b.reshape(kv_shape), "ctx", axis=1, tiled=True),
    )
    grad_full = grad_out.reshape(tokens, full_width)
    grad_float = grad_full.astype(jnp.float32)
    bias_grad = jnp.sum(grad_float, axis=0)
    down_grad = contract_first(grad_full, hidden_b)
    pre_grad = jnp.dot(grad_full, w_down, preferred_element_type=jnp.float32) * gelu_slope(pre_act)
    up_bias_grad = jnp.sum(pre_grad, axis=0, keepdims=True)
    pre_grad_b = pre_grad.astype(jnp.bfloat16)
    up_grad = contract_first(acts_two, pre_grad_b)
    norm_two_grad = contract_last(pre_grad_b, w_up)
    input_two, gain_two_grad, shift_two_grad = norm_backward(
        norm_two_grad, hat_two, inv_two, gain_two.astype(jnp.float32)
    )
    up_grad, down_grad, up_bias_grad, bias_grad, gain_two_grad, shift_two_grad = (
        lax.psum_scatter(up_grad, "shard", scatter_dimension=0, tiled=True),
        lax.psum_scatter(down_grad, "shard", scatter_dimension=0, tiled=True),
        lax.psum_scatter(up_bias_grad, "shard", scatter_dimension=1, tiled=True),
        lax.psum_scatter(bias_grad, "shard", scatter_dimension=0, tiled=True),
        lax.psum_scatter(gain_two_grad, "shard", scatter_dimension=0, tiled=True),
        lax.psum_scatter(shift_two_grad, "shard", scatter_dimension=0, tiled=True),
    )
    dense_grad = contract_first(grad_full, attn_out)
    out_grad = (
        jnp.dot(grad_full, w_dense, preferred_element_type=jnp.float32)
        .astype(jnp.bfloat16)
        .reshape(rows_dev, row_tokens, heads_dev, HD)
    )
    row_index = 0
    key_row = key_all[row_index].reshape(seq_len, heads_dev, HD)
    value_row = value_all[row_index].reshape(seq_len, heads_dev, HD)
    scores = row_scores(query_rows[row_index], key_row, row_index)
    prob_full = jnp.exp(scores - total_rows[row_index])
    prob_b = prob_full.astype(jnp.bfloat16)
    grad_row = out_grad[row_index]
    delta_row = jnp.sum(
        grad_row.astype(jnp.float32) * attn_heads[row_index].astype(jnp.float32), axis=-1
    ).T
    prob_grad = jnp.einsum("qhd,khd->hqk", grad_row, value_row, preferred_element_type=jnp.float32)
    score_grad = (prob_full * (prob_grad - delta_row[:, :, None])).astype(jnp.bfloat16)
    query_parts = [
        jnp.einsum("hqk,khd->qhd", score_grad, key_row, preferred_element_type=jnp.float32)
        * score_scale
    ]
    key_parts = [
        jnp.einsum(
            "hqk,qhd->khd", score_grad, query_rows[row_index], preferred_element_type=jnp.float32
        )
        * score_scale
    ]
    value_parts = [jnp.einsum("hqk,qhd->khd", prob_b, grad_row, preferred_element_type=jnp.float32)]
    all_shape = (rows_dev, seq_len // block_len, block_len, heads_dev, HD)
    key_grad, value_grad = (
        lax.psum_scatter(
            jnp.stack(key_parts, axis=0).reshape(all_shape), "ctx", scatter_dimension=1, tiled=True
        ),
        lax.psum_scatter(
            jnp.stack(value_parts, axis=0).reshape(all_shape),
            "ctx",
            scatter_dimension=1,
            tiled=True,
        ),
    )
    query_grad = rotate_back(
        jnp.stack(query_parts, axis=0).reshape(tokens, heads_dev, HD), cosine_table, sine_table
    )
    key_grad = rotate_back(key_grad.reshape(tokens, heads_dev, HD), cosine_table, sine_table)
    value_grad = value_grad.reshape(tokens, heads_dev, HD)
    proj_grad = jnp.stack([query_grad, key_grad, value_grad], axis=2).reshape(
        tokens, 3 * heads_dev * HD
    )
    qkv_bias_grad = jnp.sum(proj_grad, axis=0, keepdims=True)
    proj_grad_b = proj_grad.astype(jnp.bfloat16)
    qkv_grad = contract_first(acts_one, proj_grad_b)
    norm_one_grad = contract_last(proj_grad_b, w_qkv)
    input_one, gain_one_grad, shift_one_grad = norm_backward(
        norm_one_grad, hat_one, inv_one, gain_one.astype(jnp.float32)
    )
    qkv_grad, qkv_bias_grad, dense_grad, gain_one_grad, shift_one_grad = (
        lax.psum_scatter(qkv_grad, "shard", scatter_dimension=0, tiled=True),
        lax.psum_scatter(qkv_bias_grad, "shard", scatter_dimension=1, tiled=True),
        lax.psum_scatter(dense_grad, "shard", scatter_dimension=0, tiled=True),
        lax.psum_scatter(gain_one_grad, "shard", scatter_dimension=0, tiled=True),
        lax.psum_scatter(shift_one_grad, "shard", scatter_dimension=0, tiled=True),
    )
    input_partial = (input_one + input_two).reshape(rows_dev, groups_dev, block_len, full_width)
    input_sum = lax.psum_scatter(input_partial, "tp", scatter_dimension=3, tiled=True)
    grad_slice = lax.dynamic_slice_in_dim(grad_out, tp_rank * slice_width, slice_width, 3).astype(
        jnp.float32
    )
    input_grad = grad_slice + input_sum
    up_grad, down_grad, up_bias_grad, bias_grad, qkv_grad, qkv_bias_grad, dense_grad = lax.psum(
        (up_grad, down_grad, up_bias_grad, bias_grad, qkv_grad, qkv_bias_grad, dense_grad), "ctx"
    )
    gain_one_grad, shift_one_grad, gain_two_grad, shift_two_grad = lax.psum(
        (gain_one_grad, shift_one_grad, gain_two_grad, shift_two_grad), ("ctx", "tp")
    )
    return (
        output,
        input_grad,
        gain_one_grad,
        shift_one_grad,
        qkv_grad,
        qkv_bias_grad,
        dense_grad,
        bias_grad,
        gain_two_grad,
        shift_two_grad,
        up_grad,
        up_bias_grad,
        down_grad,
    )


def solution(mesh):
    return jax.shard_map(
        local,
        mesh=mesh,
        in_specs=(
            P("shard", "ctx", None, None),
            P("shard", "ctx", None, None),
            P("shard", None),
            P(),
            P("shard"),
            P("shard"),
            P("shard", "tp"),
            P("tp", "shard"),
            P("shard", "tp"),
            P("shard"),
            P("shard"),
            P("shard"),
            P("shard", "tp"),
            P("tp", "shard"),
            P("shard", "tp"),
            P("shard"),
        ),
        out_specs=(
            P("shard", "ctx", None, "tp"),
            P("shard", "ctx", None, "tp"),
            P("shard"),
            P("shard"),
            P("shard", "tp"),
            P("tp", "shard"),
            P("shard", "tp"),
            P("shard"),
            P("shard"),
            P("shard"),
            P("shard", "tp"),
            P("tp", "shard"),
            P("shard", "tp"),
        ),
        check_vma=False,
    )
```

profile of v0, /device:TPU:0, one launch (start us, length us, event | category | flops | bytes accessed | tf_op | source)
XLA Modules:
  0.0 1366.5 jit_solution(17029670118157438913)
XLA Ops:
  12.1 2.8 convert_reduce_fusion.1
  15.0 3.4 multiply_reduce_fusion.4
  18.4 9.9 all-gather.3
  28.3 8.4 all-gather.2
  36.7 7.3 all-gather.1
  44.0 8.1 all-gather
  52.1 8.1 all_gather.53
  61.3 6.2 gather_fusion.2
  69.7 6.3 add_convert_fusion.2
  76.1 6.8 all-gather.13.cloned.1.call-done
  82.9 11.7 convolution_add_fusion
  94.6 6.6 copy.56
  101.1 4.8 fusion.38
  108.1 2.9 copy.89
  113.1 2.3 slice_negate_fusion.2
  118.6 6.2 gather_fusion
  124.8 11.8 gather_fusion.1
  136.5 3.5 compare_and_fusion
  140.1 6.2 convolution_convert_fusion
  146.3 2.7 slice.152
  150.3 2.3 copy.57
  152.7 12.9 fusion.1
  165.6 8.5 exponential_reduce_fusion
  174.2 11.0 multiply_reduce_fusion.7
  185.2 9.9 convolution_bitcast_fusion.1
  195.2 12.6 multiply_convert_fusion
  207.8 7.9 multiply_bitcast_fusion
  215.7 5.3 copy.78
  221.0 5.4 copy.79
  227.8 6.6 convolution_bitcast_fusion.2
  236.0 6.4 add_convert_fusion
  242.5 5.7 multiply_bitcast_fusion.1
  250.1 14.5 %all-reduce.17.cloned.1.call-done = (f32[1,4,512,2,256]{4,2,1,3,0:T(8,128)}, f32[1,4,512,2,256]{4,2,1,3,0:T(8,128)}) async-done(((f32[1,4,512,2,256]{4,2,1,3,0:T(8,128)}, f32[1,4,512,2,256]{4,2,1,3,0:T(8,128)}), (f32[1,4,512,2,256]{4,2,1,3,0:T(8,128)}, f32[1,4,512,2,256]{4,2,1,3,0:T(8,128)})) %all-reduce.17.cloned.1.call-update) | async-done | bytes 8388624
  272.9 3.0 copy.68
  276.0 13.3 fusion.41
  290.0 8.6 all_gather.60
  298.6 56.4 %all-gather.21.cloned.1.call-done = bf16[2048,2048]{1,0:T(8,128)(2,1)} async-done(((bf16[512,2048]{1,0:T(8,128)(2,1)}), bf16[2048,2048]{1,0:T(8,128)(2,1)}) %all-gather.21.cloned.1.call-update) | async-done | bytes 8388624 | tf_op jit(solution)/shard_map/all_gather | solution.py:128
  355.0 30.9 %fusion.4 = (bf16[1024,2048]{1,0:T(8,128)(2,1)}, f32[1024,2048]{1,0:T(8,128)}) fusion(f32[2048]{0:T(1024)S(1)} %bitcast.201, bf16[1024,2048]{1,0:T(8,128)(2,1)} %get-tuple-element.87, bf16[2048,2048]{1,0:T(8,128)(2,1)} %all-gather.21.cloned.1.call-done), kind=kOutput, calls=%fused_computation.14 | convolution fusion | flops 8728346624 | bytes 25174016 | tf_op jit(solution)/shard_map/dot_general | solution.py:189
  385.9 58.5 %all-gather.23.cloned.1.call-done = bf16[2048,2048]{1,0:T(8,128)(2,1)} async-done(((bf16[512,2048]{1,0:T(8,128)(2,1)}), bf16[2048,2048]{1,0:T(8,128)(2,1)}) %all-gather.23.cloned.1.call-update) | async-done | bytes 8388624 | tf_op jit(solution)/shard_map/all_gather | solution.py:130
  444.4 16.3 %fusion.39 = (f32[2048]{0:T(1024)S(1)}, bf16[1024,2048]{1,0:T(8,128)(2,1)S(1)}) fusion(f32[1024,2048]{1,0:T(8,128)} %get-tuple-element.111, f32[2048]{0:T(1024)S(1)} %bitcast.202, bf16[1024,2048]{1,0:T(8,128)(2,1)} %bitcast.163, bf16[2048,2048]{1,0:T(8,128)(2,1)} %all-gather.23.cloned.1.call-done), kind=kOutput, calls=%fused_computation.128 | convolution fusion | flops 8615098368 | bytes 25182208 | tf_op jit(solution)/shard_map/dot_general | solution.py:226
  462.7 12.0 fusion.20
  474.8 15.3 %convolution_bitcast_fusion = f32[2048,2048]{0,1:T(8,128)} fusion(bf16[1024,2048]{1,0:T(8,128)(2,1)} %get-tuple-element.110, bf16[1024,2048]{1,0:T(8,128)(2,1)} %bitcast.164), kind=kOutput, calls=%fused_computation.11 | convolution fusion | flops 8589934592 | bytes 25165824 | tf_op jit(solution)/shard_map/dot_general | solution.py:79
  491.7 14.9 %fusion.40 = f32[1024,2048]{1,0:T(8,128)} fusion(bf16[1024,2048]{1,0:T(8,128)(2,1)} %get-tuple-element.110, bf16[2048,2048]{1,0:T(8,128)(2,1)} %all-gather.23.cloned.1.call-done), kind=kOutput, calls=%fused_computation.129 | convolution fusion | flops 8589934592 | bytes 20971520 | tf_op jit(solution)/shard_map/dot_general | solution.py:85
  508.5 10.7 convolution_add_fusion.1
  519.5 15.2 %fusion.22 = f32[1024,2048]{1,0:T(8,128)} fusion(bf16[2048,2048]{1,0:T(8,128)(2,1)} %all-gather.21.cloned.1.call-done, bf16[1024,2048]{1,0:T(8,128)(2,1)} %copy-done.37), kind=kOutput, calls=%fused_computation.66 | convolution fusion | flops 8589934592 | bytes 20971520 | tf_op jit(solution)/shard_map/dot_general | solution.py:85
  534.7 16.7 %multiply_reduce_fusion.1 = (f32[2048]{0:T(1024)S(1)}, f32[1024]{0:T(1024)S(1)}, f32[1024]{0:T(1024)S(1)}, f32[2048]{0:T(1024)S(1)}, f32[2048]{0:T(1024)S(1)}, /...) fusion(bf16[1,2,512,2048]{3,2,1,0:T(8,128)(2,1)S(1)} %copy-done.1, ...), kind=kOutput, calls=%fused_computation.26 | convolution fusion | flops 6478090240 | bytes 30482432 | tf_op jit(solution)/shard_map/dot_general | solution.py:85
  551.4 10.4 add_multiply_fusion
  561.9 61.8 %reduce-scatter.23.cloned.1.call-done = f32[512,1536]{1,0:T(8,128)} async-done(((f32[2048,1536]{1,0:T(8,128)}), f32[512,1536]{1,0:T(8,128)}) %reduce-scatter.23.cloned.1.call-update) | async-done | bytes 3145744 | tf_op jit(solution)/shard_map/reduce_scatter | solution.py:299
  623.7 156.7 %reduce-scatter.27.cloned.1.call-done = f32[512,2048]{1,0:T(8,128)} async-done(((f32[2048,2048]{1,0:T(8,128)}), f32[512,2048]{1,0:T(8,128)}) %reduce-scatter.27.cloned.1.call-update) | async-done | bytes 4194320 | tf_op jit(solution)/shard_map/reduce_scatter | solution.py:235
  780.4 156.8 %reduce-scatter.29.cloned.1.call-done = f32[512,2048]{0,1:T(8,128)} async-done(((f32[2048,2048]{0,1:T(8,128)}), f32[512,2048]{0,1:T(8,128)}) %reduce-scatter.29.cloned.1.call-update) | async-done | bytes 4194320 | tf_op jit(solution)/shard_map/reduce_scatter | solution.py:236
  938.5 8.0 all-gather.5
  946.6 7.4 all-gather.4
  954.1 2.9 convert_reduce_fusion
  956.9 11.6 reduce-scatter.33.cloned.1.call-done
  969.6 16.5 %all-reduce.8 = (f32[2048]{0:T(1024)S(1)}, f32[2048]{0:T(1024)S(1)}, f32[2048]{0:T(1024)S(1)}, f32[2048]{0:T(1024)S(1)}, f32[2048]{0:T(1024)S(1)}) all-reduce(f32[2048]{0:T(1024)S(1)} %get-tuple-element.54, f32[2048]{0:T(1024)S(1)} %get-tuple-element.59, ...), channel_id=6, replica_groups=mesh['shard'=4,'ctx'=2,'tp'=4] {'shard'}, use_global_device_ids=true, to_apply=%region_16.17.clone | all-reduce | flops 10240 | bytes 81920
  986.4 16.1 %all-reduce.7 = (f32[512]{0:T(512)}, f32[512]{0:T(512)}, f32[512]{0:T(512)}, f32[512]{0:T(512)}) all-reduce(f32[512]{0:T(512)S(1)} %dynamic-slice.5, f32[512]{0:T(512)S(1)} %dynamic-slice.7, f32[512]{0:T(512)S(1)} %dynamic-slice.11, f32[512]{0:T(512)S(1)} %dynamic-slice.13), channel_id=1, replica_groups=mesh['shard'=4,'ctx'=2,'tp'=4] {'ctx','tp'}, use_global_device_ids=true, to_apply=%region_17.18 | all-reduce | flops 2048 | bytes 16384 | tf_op jit(solution)/shard_map/psum | solution.py:314
  1003.5 4.6 all-reduce.9
  1008.1 137.3 %reduce-scatter.19.cloned.1.call-done = f32[1,2,512,512]{3,2,1,0:T(8,128)} async-done(((f32[1,2,512,2048]{3,2,1,0:T(8,128)}), f32[1,2,512,512]{3,2,1,0:T(8,128)}) %reduce-scatter.19.cloned.1.call-update) | async-done | bytes 2097168 | tf_op jit(solution)/shard_map/reduce_scatter | solution.py:195
  1145.4 3.5 add_add_fusion
  1148.9 143.9 %reduce-scatter.21.cloned.1.call-done = f32[1,2,512,512]{3,2,1,0:T(8,128)} async-done(((f32[1,2,512,2048]{3,2,1,0:T(8,128)}), f32[1,2,512,512]{3,2,1,0:T(8,128)}) %reduce-scatter.21.cloned.1.call-update) | async-done | bytes 2097168 | tf_op jit(solution)/shard_map/reduce_scatter | solution.py:306
  1292.9 3.5 convert_add_fusion
  1296.4 50.0 %all-reduce.15.cloned.1.call-done = (f32[512,1536]{1,0:T(8,128)}, f32[512,512]{0,1:T(8,128)}, f32[512,2048]{1,0:T(8,128)}, f32[512,2048]{0,1:T(8,128)}) async-done(((f32[512,1536]{1,0:T(8,128)}, f32[512,512]{0,1:T(8,128)}, f32[512,2048]{1,0:T(8,128)}, f32[512,2048]{0,1:T(8,128)}), (f32[512,1536]{1,0:T(8,128)}, f32[512,512]{0,1:T(8,128)}, f32[512,2048]{1,0:T(8,128)}, ...) | async-done | bytes 12582928 | tf_op jit(solution)/shard_map/psum | solution.py:311
  1346.4 2.7 copy.70
  1349.1 5.3 copy.71
  (187 shorter events, 44.4 us)
Async XLA Ops:
  7.2 44.9 %copy-start.30 = (bf16[1,384]{1,0:T(2,128)(2,1)S(1)}, bf16[1,384]{1,0:T(2,128)(2,1)}, u32[]{:S(2)}) copy-start(bf16[1,384]{1,0:T(2,128)(2,1)} %param.23) | copy-start | bytes 2308
  7.2 53.1 %copy-start = (s32[1,2048]{1,0:T(1,128)S(1)}, s32[1,2048]{1,0:T(1,128)}, u32[]{:S(2)}) copy-start(s32[1,2048]{1,0:T(1,128)} %param.18) | copy-start | bytes 24580
  7.2 75.7 %all-gather.13.cloned.1.call-start = ((), (), s32[]{:S(2)}) async-start(), calls=%async_computation.8 | async-start | bytes 7864320 | tf_op jit(solution)/shard_map/all_gather | solution.py:120
  7.9 132.1 %all-gather.19.cloned.1.call-start = ((), (), s32[]{:S(2)}) async-start(), calls=%async_computation.11 | async-start | bytes 2621440 | tf_op jit(solution)/shard_map/all_gather | solution.py:122
  8.7 144.0 %all-gather.17.cloned.1.call-start = ((), (), s32[]{:S(2)}) async-start(), calls=%async_computation.10 | async-start | bytes 3145728 | tf_op jit(solution)/shard_map/all_gather | solution.py:156
  15.0 61.1 %copy-start.25 = (f32[1,4,2,128]{3,1,2,0:T(4,128)}, f32[1,4,2,128]{3,1,2,0:T(4,128)S(1)}, u32[]{:S(2)}) copy-start(f32[1,4,2,128]{3,1,2,0:T(4,128)S(1)} %copy.90) | copy-start | bytes 12292
  18.4 57.6 %copy-start.27 = (f32[1,4,2,128]{3,1,2,0:T(4,128)}, f32[1,4,2,128]{3,1,2,0:T(4,128)S(1)}, u32[]{:S(2)}) copy-start(f32[1,4,2,128]{3,1,2,0:T(4,128)S(1)} %copy.91) | copy-start | bytes 12292
  36.7 39.3 %copy-start.23 = (f32[4,1,512]{2,1,0:T(1,128)}, f32[4,1,512]{2,1,0:T(1,128)S(1)}, u32[]{:S(2)}) copy-start(f32[4,1,512]{2,1,0:T(1,128)S(1)} %convert_element_type.161) | copy-start | bytes 24580
  52.1 183.9 %copy-start.21 = (f32[4,1,512]{2,1,0:T(1,128)}, f32[4,1,512]{2,1,0:T(1,128)S(1)}, u32[]{:S(2)}) copy-start(f32[4,1,512]{2,1,0:T(1,128)S(1)} %convert_element_type.159) | copy-start | bytes 24580
  111.0 4.4 copy-start.8
  118.3 55.9 %all-gather.15.cloned.1.call-start = ((), (), s32[]{:S(2)}) async-start(), calls=%async_computation.9 | async-start | bytes 3145728 | tf_op jit(solution)/shard_map/all_gather | solution.py:157
  152.6 111.9 %all-reduce.17.cloned.1.call-start = ((), (), s32[]{:S(2)}) async-start(), calls=%async_computation.23 | async-start | bytes 16777216
  152.7 12.9 copy-start.11
  174.2 11.1 copy-start.34
  195.2 12.6 copy-start.19
  195.2 12.6 copy-start.20
  226.4 1.4 copy-start.14
  226.4 128.6 %all-gather.21.cloned.1.call-start = ((), (), s32[]{:S(2)}) async-start(), calls=%async_computation.12 | async-start | bytes 10485760 | tf_op jit(solution)/shard_map/all_gather | solution.py:128
  227.0 217.4 %all-gather.23.cloned.1.call-start = ((), (), s32[]{:S(2)}) async-start(), calls=%async_computation.13 | async-start | bytes 10485760 | tf_op jit(solution)/shard_map/all_gather | solution.py:130
  227.7 334.2 %reduce-scatter.25.cloned.1.call-start = ((), (), s32[]{:S(2)}) async-start(), calls=%async_computation.17 | async-start | bytes 5242880 | tf_op jit(solution)/shard_map/reduce_scatter | solution.py:301
  227.8 6.7 copy-start.36
  234.4 8.0 copy-start.33
  234.4 389.3 %reduce-scatter.23.cloned.1.call-start = ((), (), s32[]{:S(2)}) async-start(), calls=%async_computation.16 | async-start | bytes 15728640 | tf_op jit(solution)/shard_map/reduce_scatter | solution.py:299
  248.2 1.3 copy-start.9
  264.5 2.8 copy-start.18
  264.5 3.5 copy-start.10
  268.0 2.9 copy-start.2
  270.3 1.3 copy-start.4
  270.9 1.4 copy-start.6
  289.3 0.7 copy-start.29
  289.3 491.1 %reduce-scatter.27.cloned.1.call-start = ((), (), s32[]{:S(2)}) async-start(), calls=%async_computation.18 | async-start | bytes 20971520 | tf_op jit(solution)/shard_map/reduce_scatter | solution.py:235
  444.4 18.3 %copy-start.13 = (bf16[1024,2048]{1,0:T(8,128)(2,1)S(1)}, bf16[1024,2048]{1,0:T(8,128)(2,1)}, u32[]{:S(2)}) copy-start(bf16[1024,2048]{1,0:T(8,128)(2,1)} %get-tuple-element.87) | copy-start | bytes 12582916
  460.7 2.0 copy-start.37
  474.7 462.5 %reduce-scatter.29.cloned.1.call-start = ((), (), s32[]{:S(2)}) async-start(), calls=%async_computation.19 | async-start | bytes 20971520 | tf_op jit(solution)/shard_map/reduce_scatter | solution.py:236
  490.1 478.4 %reduce-scatter.33.cloned.1.call-start = ((), (), s32[]{:S(2)}) async-start(), calls=%async_computation.21 | async-start | bytes 1310720
  491.6 15.0 %copy-start.3 = (f32[1,2,512,2,256]{4,2,1,3,0:T(8,128)S(1)}, f32[1,2,512,2,256]{4,2,1,3,0:T(8,128)}, u32[]{:S(2)}) copy-start(f32[1,2,512,2,256]{4,2,1,3,0:T(8,128)} %copy-done.2) | copy-start | bytes 6291460
  491.6 510.9 %reduce-scatter.31.cloned.1.call-start = ((), (), s32[]{:S(2)}) async-start(), calls=%async_computation.20 | async-start | bytes 983040
  491.6 14.9 %copy-start.5 = (f32[1024,2,1,256]{3,0,1,2:T(8,128)S(1)}, f32[1024,2,1,256]{3,0,1,2:T(8,128)}, u32[]{:S(2)}) copy-start(f32[1024,2,1,256]{3,0,1,2:T(8,128)} %copy-done.4) | copy-start | bytes 6291460
  491.6 14.9 %copy-start.7 = (f32[1024,2,1,256]{3,0,1,2:T(8,128)S(1)}, f32[1024,2,1,256]{3,0,1,2:T(8,128)}, u32[]{:S(2)}) copy-start(f32[1024,2,1,256]{3,0,1,2:T(8,128)} %copy-done.6) | copy-start | bytes 6291460
  506.6 2.0 copy-start.15
  508.5 636.9 %reduce-scatter.19.cloned.1.call-start = ((), (), s32[]{:S(2)}) async-start(), calls=%async_computation.14 | async-start | bytes 10485760 | tf_op jit(solution)/shard_map/reduce_scatter | solution.py:195
  519.2 15.4 %copy-start.17 = (bf16[1024,2,3,256]{0,3,2,1:T(8,128)(2,1)S(1)}, bf16[1024,2,3,256]{0,3,2,1:T(8,128)(2,1)}, u32[]{:S(2)}) copy-start(bf16[1024,2,3,256]{0,3,2,1:T(8,128)(2,1)} %copy.68) | copy-start | bytes 9437188
  519.3 15.4 %copy-start.22 = (f32[4,1,512]{2,1,0:T(1,128)S(1)}, f32[4,1,512]{2,1,0:T(1,128)}, u32[]{:S(2)}) copy-start(f32[4,1,512]{2,1,0:T(1,128)} %copy-done.21) | copy-start | bytes 24580
  519.3 15.4 %copy-start.24 = (f32[4,1,512]{2,1,0:T(1,128)S(1)}, f32[4,1,512]{2,1,0:T(1,128)}, u32[]{:S(2)}) copy-start(f32[4,1,512]{2,1,0:T(1,128)} %copy-done.23) | copy-start | bytes 24580
  519.3 15.4 %copy-start.26 = (f32[1,4,2,128]{3,1,2,0:T(4,128)S(1)}, f32[1,4,2,128]{3,1,2,0:T(4,128)}, u32[]{:S(2)}) copy-start(f32[1,4,2,128]{3,1,2,0:T(4,128)} %copy-done.25) | copy-start | bytes 12292
  519.3 15.4 %copy-start.28 = (f32[1,4,2,128]{3,1,2,0:T(4,128)S(1)}, f32[1,4,2,128]{3,1,2,0:T(4,128)}, u32[]{:S(2)}) copy-start(f32[1,4,2,128]{3,1,2,0:T(4,128)} %copy-done.27) | copy-start | bytes 12292
  519.3 773.6 %reduce-scatter.21.cloned.1.call-start = ((), (), s32[]{:S(2)}) async-start(), calls=%async_computation.15 | async-start | bytes 10485760 | tf_op jit(solution)/shard_map/reduce_scatter | solution.py:306
  519.5 15.2 %copy-start.1 = (bf16[1,2,512,2048]{3,2,1,0:T(8,128)(2,1)S(1)}, bf16[1,2,512,2048]{3,2,1,0:T(8,128)(2,1)}, u32[]{:S(2)}) copy-start(bf16[1,2,512,2048]{3,2,1,0:T(8,128)(2,1)} %param.16) | copy-start | bytes 12582916
  561.8 375.4 %copy-start.35 = (u32[32]{0:T(128)S(1)}, u32[32]{0:T(128)}, u32[]{:S(2)}) copy-start(u32[32]{0:T(128)} %constant.136) | copy-start | bytes 388
  561.8 376.0 %copy-start.31 = (bf16[512]{0:T(512)(128)(2,1)S(1)}, bf16[512]{0:T(512)(128)(2,1)}, u32[]{:S(2)}) copy-start(bf16[512]{0:T(512)(128)(2,1)} %param.25) | copy-start | bytes 3076
  561.9 376.0 %copy-start.32 = (bf16[512]{0:T(512)(128)(2,1)S(1)}, bf16[512]{0:T(512)(128)(2,1)}, u32[]{:S(2)}) copy-start(bf16[512]{0:T(512)(128)(2,1)} %param.31) | copy-start | bytes 3076
  561.9 784.5 %all-reduce.15.cloned.1.call-start = ((), (), s32[]{:S(2)}) async-start(), calls=%async_computation.22 | async-start | bytes 25165824 | tf_op jit(solution)/shard_map/psum | solution.py:311
  1346.4 8.0 copy-start.16
  1354.4 3.3 copy-start.12
Sparse Core Ops, SparseCore 0:
  9.9 72.9 all-gather.12
  84.7 35.1 all-gather.18
  122.1 10.5 all-gather.16
  152.7 10.7 all-gather.14
  226.5 37.9 all-reduce.16
  266.2 88.7 all-gather.20
  356.9 87.4 all-gather.22
  447.4 52.5 reduce-scatter.24
  503.1 120.6 reduce-scatter.22
  626.6 153.7 reduce-scatter.26
  783.5 153.7 reduce-scatter.28
  940.5 27.9 reduce-scatter.32
  972.0 26.4 reduce-scatter.30
  1000.7 144.6 reduce-scatter.18
  1147.6 145.2 reduce-scatter.20
  1295.5 50.8 all-reduce.14
where the time goes:
time: 1370 us
  waiting for transfers between devices  857 us (63%)
  matrix products  230 us (17%)
  blocking collectives  103 us (8%)
  local copies, waits for them, and re-layouts  95.1 us (7%)
  other arithmetic  64.2 us (5%)
  between operations  16.5 us (1%)
    reduce_scatter x1, waiting for transfers between devices, local(): lax.psum_scatter(down_grad, 'shard', scatter_dimension=0, tiled=True)  157 us
    reduce_scatter x1, waiting for transfers between devices, local(): lax.psum_scatter(up_grad, 'shard', scatter_dimension=0, tiled=True)  157 us
    reduce_scatter x1, waiting for transfers between devices, local(): lax.psum_scatter(input_partial, 'tp', scatter_dimension=3, tiled=True)  144 us
    reduce_scatter x1, waiting for transfers between devices, local(): lax.psum_scatter(partial_out, 'tp', scatter_dimension=3, tiled=True)  137 us
    reduce_scatter x1, waiting for transfers between devices, local(): lax.psum_scatter(qkv_grad, 'shard', scatter_dimension=0, tiled=True)  61.8 us
    all_gather x1, waiting for transfers between devices, local(): lax.all_gather(down_weight, 'shard', axis=0, tiled=True)  58.5 us
    dot_general x4, matrix products, contract_last(): lax.dot_general(left_mat, right_mat, (((1,), (1,)), ((), ())), preferred_...  57.4 us
    all_gather x1, waiting for transfers between devices, local(): lax.all_gather(up_weight, 'shard', axis=0, tiled=True)  56.4 us
  transfers between devices with their start and end apart: 16, of which 11 were waited for; matrix products, arithmetic and copies ran while one was open for 23% of the time, Pallas kernels for 0%

commit v1 on v0

v1 whole, which is shorter than its diff:
```python
import functools
import math

import jax
import jax.numpy as jnp
from jax import lax
from jax.experimental import pallas as pl
from jax.experimental.pallas import tpu as pltpu
from jax.sharding import PartitionSpec as P

HD = 256
ROT = 64
LANES = 128

EPSILON = 1e-05
ROTARY_BASE = 10000.0
NEG = -1e30
VMEM_LIMIT = 56 * 1024 * 1024


def segment_positions(segments):
    length_all = segments.shape[0]
    index_row = jnp.arange(length_all, dtype=jnp.int32)
    changed = jnp.concatenate(
        [jnp.ones((1,), dtype=jnp.bool_), segments[1:] != segments[:-1]]
    )
    seg_start = jnp.where(changed, index_row, jnp.zeros_like(segments))
    return index_row - lax.cummax(seg_start, axis=0)


def rotary_tables(positions):
    half_rot = ROT // 2
    frequency = ROTARY_BASE ** (-2.0 * jnp.arange(half_rot, dtype=jnp.float32) / ROT)
    angles = positions.astype(jnp.float32)[:, None] * frequency[None, :]
    cosine, sine = jnp.cos(angles), jnp.sin(angles)
    count = positions.shape[0]
    rest_one = jnp.ones((count, LANES - ROT), jnp.float32)
    rest_zero = jnp.zeros((count, LANES - half_rot), jnp.float32)
    cosine_table = jnp.concatenate([cosine, cosine, rest_one], axis=1)
    low_table = jnp.concatenate([-sine, rest_zero], axis=1)
    high_table = jnp.concatenate(
        [jnp.zeros_like(sine), sine, rest_zero[:, : LANES - ROT]], axis=1
    )
    return cosine_table, low_table, high_table


def turn(values, cosine, low, high, sign):
    half_rot = ROT // 2
    down = pltpu.roll(values, LANES - half_rot, 1)
    up = pltpu.roll(values, half_rot, 1)
    return values * cosine + sign * (down * low + up * high)


def contract_first(left_mat, right_mat):
    return lax.dot_general(
        left_mat, right_mat, (((0,), (0,)), ((), ())), preferred_element_type=jnp.float32
    )


def contract_last(left_mat, right_mat):
    return lax.dot_general(
        left_mat, right_mat, (((1,), (1,)), ((), ())), preferred_element_type=jnp.float32
    )


def block_meets(bounds_ref, order_ref, q_index, k_index):
    return (
        (order_ref[k_index] <= order_ref[q_index])
        & (bounds_ref[0, k_index] <= bounds_ref[1, q_index])
        & (bounds_ref[1, k_index] >= bounds_ref[0, q_index])
    )


def pair_mask(order_ref, seg_col_ref, seg_row_ref, q_index, k_index, block):
    q_place = order_ref[q_index] * block + lax.broadcasted_iota(jnp.int32, (block, block), 0)
    k_place = order_ref[k_index] * block + lax.broadcasted_iota(jnp.int32, (block, block), 1)
    seg_q = seg_col_ref[pl.ds(q_index * block, block), :]
    seg_k = seg_row_ref[:, pl.ds(pl.multiple_of(k_index * block, block), block)]
    return (k_place <= q_place) & (seg_q == seg_k)


def attend_kernel(
    order_ref,
    bounds_ref,
    proj_ref,
    cos_ref,
    low_ref,
    high_ref,
    seg_col_ref,
    seg_row_ref,
    query_ref,
    key_ref,
    value_ref,
    attn_ref,
    lse_ref,
    top_ref,
    sum_ref,
    acc_ref,
    *,
    block,
    count,
):
    score_scale = 1.0 / math.sqrt(HD)
    for index in range(count):
        rows = pl.ds(index * block, block)
        tables = (cos_ref[rows, :], low_ref[rows, :], high_ref[rows, :])
        for start, out in ((0, query_ref), (HD, key_ref)):
            out[rows, :LANES] = turn(
                proj_ref[rows, start : start + LANES], *tables, 1.0
            ).astype(jnp.bfloat16)
            out[rows, LANES:] = proj_ref[rows, start + LANES : start + HD].astype(jnp.bfloat16)
        value_ref[rows, :] = proj_ref[rows, 2 * HD :].astype(jnp.bfloat16)

    @pl.loop(0, count)
    def _(q_index):
        rows = pl.ds(pl.multiple_of(q_index * block, block), block)
        top_ref[...] = jnp.full_like(top_ref, NEG)
        sum_ref[...] = jnp.zeros_like(sum_ref)
        acc_ref[...] = jnp.zeros_like(acc_ref)

        @pl.loop(0, count)
        def _(k_index):
            @pl.when(block_meets(bounds_ref, order_ref, q_index, k_index))
            def _():
                keys = pl.ds(pl.multiple_of(k_index * block, block), block)
                scores = contract_last(query_ref[rows, :], key_ref[keys, :]) * score_scale
                allowed = pair_mask(order_ref, seg_col_ref, seg_row_ref, q_index, k_index, block)
                scores = jnp.where(allowed, scores, NEG)
                old_top = top_ref[...]
                new_top = jnp.maximum(old_top, jnp.max(scores, axis=1, keepdims=True))
                shrink = jnp.exp(old_top - new_top)
                weights = jnp.where(allowed, jnp.exp(scores - new_top), 0.0)
                top_ref[...] = new_top
                sum_ref[...] = sum_ref[...] * shrink + jnp.sum(weights, axis=1, keepdims=True)
                acc_ref[...] = acc_ref[...] * shrink + jnp.dot(
                    weights.astype(jnp.bfloat16),
                    value_ref[keys, :],
                    preferred_element_type=jnp.float32,
                )

        attn_ref[rows, :] = (acc_ref[...] / sum_ref[...]).astype(jnp.bfloat16)
        lse_ref[rows, :] = top_ref[...] + jnp.log(sum_ref[...])


def attend_grad_kernel(
    order_ref,
    bounds_ref,
    query_ref,
    key_ref,
    value_ref,
    attn_ref,
    grad_ref,
    lse_ref,
    cos_ref,
    low_ref,
    high_ref,
    seg_col_ref,
    seg_row_ref,
    out_ref,
    sums_ref,
    query_acc,
    key_acc,
    value_acc,
    delta_ref,
    *,
    block,
    count,
):
    score_scale = 1.0 / math.sqrt(HD)
    query_acc[...] = jnp.zeros_like(query_acc)
    delta_ref[...] = jnp.sum(
        grad_ref[...].astype(jnp.float32) * attn_ref[...].astype(jnp.float32),
        axis=1,
        keepdims=True,
    )

    @pl.loop(0, count)
    def _(k_index):
        keys = pl.ds(pl.multiple_of(k_index * block, block), block)
        key_acc[...] = jnp.zeros_like(key_acc)
        value_acc[...] = jnp.zeros_like(value_acc)

        @pl.loop(0, count)
        def _(q_index):
            @pl.when(block_meets(bounds_ref, order_ref, q_index, k_index))
            def _():
                rows = pl.ds(pl.multiple_of(q_index * block, block), block)
                query, key_rows = query_ref[rows, :], key_ref[keys, :]
                grad_rows = grad_ref[rows, :]
                scores = contract_last(query, key_rows) * score_scale
                allowed = pair_mask(order_ref, seg_col_ref, seg_row_ref, q_index, k_index, block)
                probs = jnp.where(allowed, jnp.exp(scores - lse_ref[rows, :]), 0.0)
                prob_grad = contract_last(grad_rows, value_ref[keys, :])
                score_grad = (probs * (prob_grad - delta_ref[rows, :])).astype(jnp.bfloat16)
                value_acc[...] += contract_first(probs.astype(jnp.bfloat16), grad_rows)
                key_acc[...] += contract_first(score_grad, query)
                query_acc[rows, :] += jnp.dot(
                    score_grad, key_rows, preferred_element_type=jnp.float32
                )

        tables = (cos_ref[keys, :], low_ref[keys, :], high_ref[keys, :])
        key_low = turn(key_acc[:, :LANES] * score_scale, *tables, -1.0)
        key_high = key_acc[:, LANES:] * score_scale
        first = k_index == 0
        for start, part in ((HD, key_low), (HD + LANES, key_high), (2 * HD, value_acc[...])):
            columns = slice(start, start + part.shape[1])
            out_ref[keys, columns] = part.astype(jnp.bfloat16)
            sums_ref[:, columns] = jnp.where(first, 0.0, sums_ref[:, columns]) + jnp.sum(
                part, axis=0, keepdims=True
            )

    sums_ref[:, :HD] = jnp.zeros((1, HD), jnp.float32)

    @pl.loop(0, count)
    def _(q_index):
        rows = pl.ds(pl.multiple_of(q_index * block, block), block)
        tables = (cos_ref[rows, :], low_ref[rows, :], high_ref[rows, :])
        query_low = turn(query_acc[rows, :LANES] * score_scale, *tables, -1.0)
        query_high = query_acc[rows, LANES:] * score_scale
        for start, part in ((0, query_low), (LANES, query_high)):
            columns = slice(start, start + part.shape[1])
            out_ref[rows, columns] = part.astype(jnp.bfloat16)
            sums_ref[:, columns] += jnp.sum(part, axis=0, keepdims=True)


SCALAR = pl.BlockSpec(memory_space=pltpu.SMEM)
VECTOR = pl.BlockSpec(memory_space=pltpu.VMEM)


def attend(order, bounds, proj, tables, seg_col, seg_row, block, count):
    length = proj.shape[0]
    pairs = length * length
    return pl.pallas_call(
        functools.partial(attend_kernel, block=block, count=count),
        out_shape=(
            jax.ShapeDtypeStruct((length, HD), jnp.bfloat16),
            jax.ShapeDtypeStruct((length, HD), jnp.bfloat16),
            jax.ShapeDtypeStruct((length, HD), jnp.bfloat16),
            jax.ShapeDtypeStruct((length, HD), jnp.bfloat16),
            jax.ShapeDtypeStruct((length, 1), jnp.float32),
        ),
        in_specs=[SCALAR] * 2 + [VECTOR] * 6,
        out_specs=(VECTOR,) * 5,
        scratch_shapes=[
            pltpu.VMEM((block, 1), jnp.float32),
            pltpu.VMEM((block, 1), jnp.float32),
            pltpu.VMEM((block, HD), jnp.float32),
        ],
        compiler_params=pltpu.CompilerParams(vmem_limit_bytes=VMEM_LIMIT),
        cost_estimate=pl.CostEstimate(
            flops=2 * pairs * HD, bytes_accessed=16 * length * HD, transcendentals=pairs // 2
        ),
        name="attend",
    )(order, bounds, proj, *tables, seg_col, seg_row)


def attend_grad(
    order, bounds, query, key, value, attn, grad, lse, tables, seg_col, seg_row, block, count
):
    length = query.shape[0]
    pairs = length * length
    return pl.pallas_call(
        functools.partial(attend_grad_kernel, block=block, count=count),
        out_shape=(
            jax.ShapeDtypeStruct((length, 3 * HD), jnp.bfloat16),
            jax.ShapeDtypeStruct((1, 3 * HD), jnp.float32),
        ),
        in_specs=[SCALAR] * 2 + [VECTOR] * 11,
        out_specs=(VECTOR,) * 2,
        scratch_shapes=[
            pltpu.VMEM((length, HD), jnp.float32),
            pltpu.VMEM((block, HD), jnp.float32),
            pltpu.VMEM((block, HD), jnp.float32),
            pltpu.VMEM((length, 1), jnp.float32),
        ],
        compiler_params=pltpu.CompilerParams(vmem_limit_bytes=VMEM_LIMIT),
        cost_estimate=pl.CostEstimate(
            flops=5 * pairs * HD, bytes_accessed=16 * length * HD, transcendentals=pairs // 2
        ),
        name="attend_grad",
    )(order, bounds, query, key, value, attn, grad, lse, *tables, seg_col, seg_row)


def ring_shift(value, axis, step):
    count = lax.axis_size(axis)
    return lax.ppermute(value, axis, [(i, (i + step) % count) for i in range(count)])


def local(
    hidden_in,
    grad_out,
    segment_ids,
    group_order,
    ln1_gain,
    ln1_bias,
    qkv_weight,
    qkv_bias,
    dense_weight,
    dense_bias,
    ln2_gain,
    ln2_bias,
    up_weight,
    up_bias,
    down_weight,
    down_bias,
):
    _, groups_dev, block_len, width = hidden_in.shape
    tokens = groups_dev * block_len
    seq_len = segment_ids.shape[1]
    groups = seq_len // block_len
    ctx_count, tp_count = lax.axis_size("ctx"), lax.axis_size("tp")
    shard_count = lax.axis_size("shard")
    ctx_rank, tp_rank = lax.axis_index("ctx"), lax.axis_index("tp")
    shard_rank = lax.axis_index("shard")
    slice_width = width // tp_count
    bf16, f32 = jnp.bfloat16, jnp.float32

    def my_columns(matrix):
        columns = matrix.shape[1] // ctx_count
        return lax.dynamic_slice_in_dim(matrix, ctx_rank * columns, columns, 1)

    def gather_rows(matrix):
        return lax.all_gather(my_columns(matrix), "shard", axis=0, tiled=True)

    def whole_row(part):
        return jnp.concatenate(
            [part] + [ring_shift(part, "ctx", ctx_count - k) for k in range(1, ctx_count)], axis=0
        )

    x_mine = hidden_in.reshape(tokens, width)
    g_mine = grad_out.reshape(tokens, width)
    x_row = whole_row(x_mine)
    g_row = whole_row(g_mine)

    vectors = [
        ln1_gain, ln1_bias, ln2_gain, ln2_bias, dense_bias, down_bias, qkv_bias[0], up_bias[0],
    ]
    sizes = [v.shape[0] for v in vectors]
    packed = lax.all_gather(jnp.concatenate(vectors)[None], "shard", axis=0, tiled=True)
    spread, offset = [], 0
    for size in sizes:
        spread.append(packed[:, offset : offset + size].reshape(-1).astype(f32))
        offset += size
    gain_one, shift_one, gain_two, shift_two, bias_dense, bias_down, bias_qkv, bias_up = spread
    bias_qkv = my_columns(bias_qkv[None])
    bias_up = my_columns(bias_up[None])

    w_qkv = gather_rows(qkv_weight)
    w_dense = gather_rows(dense_weight)
    w_up = gather_rows(up_weight)
    w_down = gather_rows(down_weight)
    heads_here = w_qkv.shape[1] // (3 * HD)

    own_order = jnp.concatenate(
        [
            lax.dynamic_slice_in_dim(
                group_order, lax.rem(ctx_rank + k, ctx_count) * groups_dev, groups_dev
            )
            for k in range(ctx_count)
        ]
    )
    segments = segment_ids[0]
    positions = segment_positions(segments)

    def stored(values):
        return jnp.concatenate(
            [
                lax.dynamic_slice_in_dim(values, own_order[k] * block_len, block_len)
                for k in range(groups)
            ]
        )

    seg_stored = stored(segments)
    tables = rotary_tables(stored(positions))
    seg_blocks = seg_stored.reshape(groups, block_len)
    bounds = jnp.stack([seg_blocks[:, 0], seg_blocks[:, -1]])
    seg_col, seg_row = seg_stored[:, None], seg_stored[None, :]

    x_float = x_row.astype(f32)
    centered = x_float - jnp.mean(x_float, axis=-1, keepdims=True)
    inverse = lax.rsqrt(jnp.mean(centered * centered, axis=-1, keepdims=True) + EPSILON)
    hat = centered * inverse
    acts_one = (hat * gain_one + shift_one).astype(bf16)
    acts_two = (hat * gain_two + shift_two).astype(bf16)

    projected = jnp.dot(acts_one, w_qkv, preferred_element_type=f32) + bias_qkv
    heads = []
    for h in range(heads_here):
        heads.append(
            attend(
                own_order,
                bounds,
                projected[:, 3 * HD * h : 3 * HD * (h + 1)],
                tables,
                seg_col,
                seg_row,
                block_len,
                groups,
            )
        )
    attn = jnp.concatenate([head[3] for head in heads], axis=1)

    pre_act = jnp.dot(acts_two, w_up, preferred_element_type=f32) + bias_up
    cdf = 0.5 * (1.0 + lax.erf(pre_act * (1.0 / math.sqrt(2.0))))
    hidden = (pre_act * cdf).astype(bf16)
    slope = cdf + pre_act * jnp.exp(-0.5 * pre_act * pre_act) * (1.0 / math.sqrt(2.0 * math.pi))

    def reduce_partial(partial):
        total = partial[:tokens]
        for k in range(1, ctx_count):
            piece = partial[k * tokens : (k + 1) * tokens].astype(bf16)
            total = total + ring_shift(piece, "ctx", k).astype(f32)
        return lax.psum_scatter(
            total.astype(bf16), "tp", scatter_dimension=1, tiled=True
        ).astype(f32)

    partial_out = contract_last(attn, w_dense) + contract_last(hidden, w_down)
    summed_out = reduce_partial(partial_out)
    out_shift = lax.dynamic_slice_in_dim(bias_dense + bias_down, tp_rank * slice_width, slice_width)
    x_slice = lax.dynamic_slice_in_dim(x_mine, tp_rank * slice_width, slice_width, 1)
    output = x_slice.astype(f32) + summed_out + out_shift

    def reduce_weight(grad):
        mine = lax.psum_scatter(grad.astype(bf16), "shard", scatter_dimension=0, tiled=True)
        rows, columns = mine.shape
        whole = jnp.zeros((rows, columns * ctx_count), f32)
        for k in range(ctx_count):
            part = mine if k == 0 else ring_shift(mine, "ctx", ctx_count - k)
            place = lax.rem(ctx_rank + k, ctx_count) * columns
            whole = lax.dynamic_update_slice_in_dim(whole, part.astype(f32), place, 1)
        return whole

    bias_grad = jnp.sum(g_row.astype(f32), axis=0)
    down_grad = reduce_weight(contract_first(g_row, hidden))
    pre_grad = jnp.dot(g_row, w_down, preferred_element_type=f32) * slope
    up_bias_grad = jnp.sum(pre_grad, axis=0)
    pre_grad_b = pre_grad.astype(bf16)
    up_grad = reduce_weight(contract_first(acts_two, pre_grad_b))
    norm_two_grad = contract_last(pre_grad_b, w_up)

    dense_grad = reduce_weight(contract_first(g_row, attn))
    attn_grad = jnp.dot(g_row, w_dense, preferred_element_type=f32).astype(bf16)
    proj_parts, sum_parts = [], []
    for h, (query, key, value, attn_head, lse) in enumerate(heads):
        part, sums = attend_grad(
            own_order,
            bounds,
            query,
            key,
            value,
            attn_head,
            attn_grad[:, HD * h : HD * (h + 1)],
            lse,
            tables,
            seg_col,
            seg_row,
            block_len,
            groups,
        )
        proj_parts.append(part)
        sum_parts.append(sums[0])
    proj_grad_b = jnp.concatenate(proj_parts, axis=1)
    qkv_bias_grad = jnp.concatenate(sum_parts)
    qkv_grad = reduce_weight(contract_first(acts_one, proj_grad_b))
    norm_one_grad = contract_last(proj_grad_b, w_qkv)

    scaled = norm_one_grad * gain_one + norm_two_grad * gain_two
    inner = (
        scaled
        - jnp.mean(scaled, axis=-1, keepdims=True)
        - hat * jnp.mean(scaled * hat, axis=-1, keepdims=True)
    )
    input_sum = reduce_partial(inverse * inner)
    g_slice = lax.dynamic_slice_in_dim(g_mine, tp_rank * slice_width, slice_width, 1)
    input_grad = g_slice.astype(f32) + input_sum

    def at_slot(vector, slot, count):
        whole = jnp.zeros((vector.shape[0] * count,), f32)
        return lax.dynamic_update_slice_in_dim(whole, vector, slot * vector.shape[0], 0)

    slot = tp_rank * ctx_count + ctx_rank
    slots = tp_count * ctx_count
    pieces = [
        at_slot(up_bias_grad, slot, slots),
        at_slot(qkv_bias_grad, slot, slots),
        jnp.where(slot == 0, bias_grad, 0.0),
        jnp.sum(norm_one_grad * hat, axis=0),
        jnp.sum(norm_one_grad, axis=0),
        jnp.sum(norm_two_grad * hat, axis=0),
        jnp.sum(norm_two_grad, axis=0),
    ]
    reduced = lax.psum(jnp.concatenate(pieces), ("shard", "ctx", "tp"))
    results, offset = [], 0
    for number, piece in enumerate(pieces):
        size = piece.shape[0]
        if number < 2:
            own = size // (tp_count * shard_count)
            start = offset + (tp_rank * shard_count + shard_rank) * own
        else:
            own = size // shard_count
            start = offset + shard_rank * own
        results.append(lax.dynamic_slice_in_dim(reduced, start, own))
        offset += size
    up_bias_grad, qkv_bias_grad, bias_grad = results[:3]
    gain_one_grad, shift_one_grad, gain_two_grad, shift_two_grad = results[3:]
    out_shape = hidden_in.shape[:3] + (slice_width,)
    return (
        output.reshape(out_shape),
        input_grad.reshape(out_shape),
        gain_one_grad,
        shift_one_grad,
        qkv_grad,
        qkv_bias_grad[None],
        dense_grad,
        bias_grad,
        gain_two_grad,
        shift_two_grad,
        up_grad,
        up_bias_grad[None],
        down_grad,
    )


def solution(mesh):
    return jax.shard_map(
        local,
        mesh=mesh,
        in_specs=(
            P("shard", "ctx", None, None),
            P("shard", "ctx", None, None),
            P("shard", None),
            P(),
            P("shard"),
            P("shard"),
            P("shard", "tp"),
            P("tp", "shard"),
            P("shard", "tp"),
            P("shard"),
            P("shard"),
            P("shard"),
            P("shard", "tp"),
            P("tp", "shard"),
            P("shard", "tp"),
            P("shard"),
        ),
        out_specs=(
            P("shard", "ctx", None, "tp"),
            P("shard", "ctx", None, "tp"),
            P("shard"),
            P("shard"),
            P("shard", "tp"),
            P("tp", "shard"),
            P("shard", "tp"),
            P("shard"),
            P("shard"),
            P("shard"),
            P("shard", "tp"),
            P("tp", "shard"),
            P("shard", "tp"),
        ),
        check_vma=False,
    )
```

time: 1370 us -> 690 us (0.50)
  waiting for transfers between devices: 857 us -> 345 us
  blocking collectives: 103 us -> 9.72 us
  matrix products: 230 us -> 164 us
  local copies, waits for them, and re-layouts: 95.1 us -> 41.5 us
  Pallas kernels: 0 us -> 35.6 us
    reduce_scatter x6, waiting for transfers between devices: 656 us -> 245 us  [the longest x2 142 us: reduce_partial(): lax.psum_scatter(total.astype(bf16), 'tp', scatter_dimension=1, tiled=True)]
    all_gather x6 -> x4, waiting for transfers between devices: 122 us -> 31.5 us  [gather_rows(): return lax.all_gather(my_columns(matrix), 'shard', axis=0, tiled=True)]
    dot_general x10 -> x4, matrix products: 125 us -> 57 us  [the longest x1 17.5 us: local(): pre_act = jnp.dot(acts_two, w_up, preferred_element_type=f32) + bias_up]
    all_gather x8 -> x1, blocking collectives: 65.8 us -> 9.72 us  [local(): lax.all_gather(jnp.concatenate(vectors)[None], 'shard', axis=0, tiled=True)]
    pallas_call x0 -> x2, Pallas kernels: none -> 35.6 us  [the longest x1 18.1 us: attend(): pl.pallas_call(functools.partial(attend_kernel, block=block, count=count)...]
    unnamed x19 -> x11, waiting for transfers between devices: 28.8 us -> 0.18 us
    gather x3 -> x0, local copies, waits for them, and re-layouts: 24.1 us -> none  [the longest x1 11.8 us: local(): seg_keys = segment_ids[:, place_all]]
    psum x2 -> x0, blocking collectives: 20.7 us -> none  [the longest x1 16.1 us: local(): lax.psum((gain_one_grad, shift_one_grad, gain_two_grad, shift_two_grad),...]
  transfers between devices with their start and end apart: 16 -> 19, of which waited for: 11 -> 9; matrix products, arithmetic and copies ran while one was open for 23% -> 37% of each run, Pallas kernels for 0% -> 5%
where the time goes in v1:
time: 690 us; the launch traced here: 683 us
  waiting for transfers between devices  345 us (50%)
  matrix products  164 us (24%)
  other arithmetic  67 us (10%)
  local copies, waits for them, and re-layouts  41.5 us (6%)
  Pallas kernels  35.6 us (5%)
  between operations  17.6 us (3%)
  blocking collectives  9.72 us (1%)
    reduce_scatter x2, waiting for transfers between devices, reduce_partial(): lax.psum_scatter(total.astype(bf16), 'tp', scatter_dimension=1, tiled=True)  142 us
    reduce_scatter x4, waiting for transfers between devices, reduce_weight(): lax.psum_scatter(grad.astype(bf16), 'shard', scatter_dimension=0, tiled=T...  104 us
    dot_general x4, matrix products, contract_last(): lax.dot_general(left_mat, right_mat, (((1,), (1,)), ((), ())), preferred_...  59.1 us
    psum x1, waiting for transfers between devices, local(): reduced = lax.psum(jnp.concatenate(pieces), ('shard', 'ctx', 'tp'))  53.5 us
    dot_general x4, matrix products, contract_first(): lax.dot_general(left_mat, right_mat, (((0,), (0,)), ((), ())), preferred_...  48.2 us
    all_gather x4, waiting for transfers between devices, gather_rows(): return lax.all_gather(my_columns(matrix), 'shard', axis=0, tiled=True)  31.5 us
    pallas_call x1, Pallas kernels, attend(): pl.pallas_call(functools.partial(attend_kernel, block=block, count=count)...  18.1 us
    dot_general x1, matrix products, local(): pre_act = jnp.dot(acts_two, w_up, preferred_element_type=f32) + bias_up  17.5 us
  transfers between devices with their start and end apart: 19, of which 9 were waited for; matrix products, arithmetic and copies ran while one was open for 37% of the time, Pallas kernels for 5%

profile of v1, /device:TPU:0, one launch (start us, length us, event | category | flops | bytes accessed | tf_op | source)
XLA Modules:
  0.0 682.7 jit_solution(14000047309606480047)
XLA Ops:
  7.4 1.8 constant_dynamic-slice_fusion.2
  9.2 2.1 constant_dynamic-slice_fusion.3
  11.4 1.1 constant_dynamic-slice_fusion.1
  13.2 2.3 constant_dynamic-slice_fusion
  15.6 0.6 fusion.39
  19.7 1.3 copy.33.seg_col_ref
  22.9 9.7 %all-gather.1 = bf16[4,1,3968]{2,1,0:T(2,128)(2,1)S(1)} all-gather(bf16[1,1,3968]{2,1,0:T(2,128)(2,1)S(1)} %reshape.186), channel_id=2, replica_groups=mesh['shard'=4,'ctx'=2,'tp'=4] {'shard'}, dimensions={0}, use_global_device_ids=true | all-gather | bytes 39680 | tf_op jit(solution)/shard_map/all_gather | solution.py:339
  33.2 3.7 multiply_sine_fusion
  37.0 1.0 concatenate.47.low_ref
  38.0 0.6 pad_add_fusion.2.order_ref
  38.8 0.6 pad_add_fusion.1.bounds_ref
  39.3 1.3 maximum_maximum_fusion.cos_ref
  40.7 1.3 maximum_maximum_fusion.1.high_ref
  42.0 4.8 convert_reduce_fusion
  46.8 6.3 fusion.17
  53.1 3.4 convert_reduce_fusion.1
  56.5 7.0 %convolution_convert_fusion.4.grad_ref = bf16[2048,256]{1,0:T(8,128)(2,1)} fusion(bf16[2048,256]{1,0:T(8,128)(2,1)} %all-gather.9.cloned.1.call-done, bf16[1024,2048]{1,0:T(8,128)(2,1)} %collective-permute-done.2, bf16[1024,2048]{1,0:T(8,128)(2,1)} %bitcast.71), kind=kOutput, calls=%fused_computation.44 | convolution fusion | flops 2164785152 | bytes 10485760 | tf_op jit(solution)/shard_map/dot_general | solution.py:442
  63.6 22.1 %all-gather.7.cloned.1.call-done = bf16[2048,768]{1,0:T(8,128)(2,1)} async-done(((bf16[512,768]{1,0:T(8,128)(2,1)}), bf16[2048,768]{1,0:T(8,128)(2,1)}) %all-gather.7.cloned.1.call-update) | async-done | bytes 3145744 | tf_op jit(solution)/shard_map/all_gather | solution.py:323
  85.7 15.2 %broadcast_add_fusion.proj_ref = f32[2048,768]{1,0:T(8,128)} fusion(f32[768]{0:T(1024)S(1)} %dynamic-slice.10, bf16[2048,768]{1,0:T(8,128)(2,1)} %all-gather.7.cloned.1.call-done, f32[2048]{0:T(1024)S(1)} %bitcast.95, f32[2048]{0:T(1024)S(1)} %bitcast.92, f32[2048]{0:T(1024)S(1)} %add_rsqrt_fusion, f32[2048]{0:T(1024)S(1)} %broadcast_multiply_fusion.2, ...), kind=kOutput, calls=%fused_computation.42 | convolution fusion | flops 6481772544 | bytes 17861632 | tf_op jit(solution)/shard_map/dot_general | solution.py:386
  100.9 18.1 %attend.1 = (bf16[2048,256]{1,0:T(8,128)(2,1)}, bf16[2048,256]{1,0:T(8,128)(2,1)}, bf16[2048,256]{1,0:T(8,128)(2,1)}, bf16[2048,256]{1,0:T(8,128)(2,1)}, f32[2048,1]{1,0:T(8,128)}) custom-call(s32[4]{0:T(128)} %pad_add_fusion.2.order_ref, s32[2,4]{1,0:T(2,128)} %pad_add_fusion.1.bounds_ref, f32[2048,768]{1,0:T(8,128)} %broadcast_add_fusion.proj_ref, ...), custom_call_target="tpu_custom_call" | custom-call | flops 2147483648 | bytes 8388608 | tf_op jit(solution)/shard_map/attend/pallas_call | solution.py:233
  119.0 6.0 convolution_convert_fusion.3
  125.1 17.5 %attend_grad.1 = (bf16[2048,768]{1,0:T(8,128)(2,1)}, f32[1,768]{1,0:T(1,128)}) custom-call(s32[4]{0:T(128)} %pad_add_fusion.2.order_ref, s32[2,4]{1,0:T(2,128)} %pad_add_fusion.1.bounds_ref, bf16[2048,256]{1,0:T(8,128)(2,1)} %get-tuple-element.21.query_ref, bf16[2048,256]{1,0:T(8,128)(2,1)} %get-tuple-element.22.key_ref, ...), custom_call_target="tpu_custom_call" | custom-call | flops 5368709120 | bytes 8388608 | tf_op jit(solution)/shard_map/attend_grad/pallas_call | solution.py:262
  142.6 12.7 %convolution_convert_fusion.2 = bf16[2048,768]{1,0:T(8,128)(2,1)} fusion(bf16[2048,768]{1,0:T(8,128)(2,1)} %get-tuple-element.25, f32[2048]{0:T(1024)S(1)} %bitcast.96, f32[2048]{0:T(1024)S(1)} %bitcast.93, f32[2048]{0:T(1024)S(1)} %add_rsqrt_fusion, f32[2048]{0:T(1024)S(1)} %broadcast_multiply_fusion.2, bf16[1024,2048]{1,0:T(8,128)(2,1)} %collective-permute-done, ...), kind=kOutput, calls=%fused_computation.41 | convolution fusion | flops 6481772544 | bytes 14712832 | tf_op jit(solution)/shard_map/dot_general | solution.py:55
  155.4 0.7 dynamic_update_slice.31
  156.1 12.5 %fusion.44 = f32[2048,2048]{1,0:T(8,128)} fusion(bf16[2048,768]{1,0:T(8,128)(2,1)} %get-tuple-element.25, bf16[2048,768]{1,0:T(8,128)(2,1)} %all-gather.7.cloned.1.call-done), kind=kOutput, calls=%fused_computation.113 | convolution fusion | flops 6442450944 | bytes 23068672 | tf_op jit(solution)/shard_map/dot_general | solution.py:61
  168.7 17.5 %multiply_convert_fusion = (bf16[2048,1024]{1,0:T(8,128)(2,1)}, f32[2048,1024]{1,0:T(8,128)}) fusion(f32[1024]{0:T(1024)S(1)} %dynamic-slice.11, bf16[2048,1024]{1,0:T(8,128)(2,1)} %all-gather.11.cloned.1.call-done, f32[2048]{0:T(1024)S(1)} %bitcast.90, f32[2048]{0:T(1024)S(1)} %bitcast.87, f32[2048]{0:T(1024)S(1)} %add_rsqrt_fusion, ...), kind=kOutput, calls=%fused_computation.37 | convolution fusion | flops 8640266240 | bytes 25202688 | tf_op jit(solution)/shard_map/dot_general | solution.py:403
  186.2 9.4 %all-gather.13.cloned.1.call-done = bf16[2048,1024]{1,0:T(8,128)(2,1)} async-done(((bf16[512,1024]{1,0:T(8,128)(2,1)}), bf16[2048,1024]{1,0:T(8,128)(2,1)}) %all-gather.13.cloned.1.call-update) | async-done | bytes 4194320 | tf_op jit(solution)/shard_map/all_gather | solution.py:323
  195.6 17.2 %fusion.42 = (f32[1024]{0:T(1024)S(1)}, bf16[2048,1024]{1,0:T(8,128)(2,1)}) fusion(f32[2048,1024]{1,0:T(8,128)} %get-tuple-element.70, f32[1024]{0:T(1024)S(1)} %dynamic-slice.11, bf16[2048,1024]{1,0:T(8,128)(2,1)} %all-gather.13.cloned.1.call-done, bf16[1024,2048]{1,0:T(8,128)(2,1)} %collective-permute-done.2, bf16[1024,2048]{1,0:T(8,128)(2,1)} %bitcast.72), kind=kOutput, calls=%fused_computation.111 | convolution fusion | flops 8631876608 | bytes 25174016 | tf_op jit(solution)/shard_map/dot_general | solution.py:435
  213.1 22.7 %fusion.34 = (f32[2048]{0:T(1024)S(1)}, f32[2048]{0:T(1024)S(1)}, f32[2048]{0:T(1024)S(1)}, f32[2048]{0:T(1024)S(1)}, f32[2048,2048]{1,0:T(8,128)}, /*index=5*/f32[2048]{0:T(1024)S(1)}, f32[2048]{0:T(1024)S(1)}) fusion(f32[2048]{0:T(1024)S(1)} %add_rsqrt_fusion, f32[2048]{0:T(1024)S(1)} %broadcast_multiply_fusion.2, ...), kind=kOutput, calls=%fused_computation.103 | convolution fusion | flops 8665419776 | bytes 50413568 | tf_op jit(solution)/shard_map/dot_general | solution.py:61
  235.9 0.6 copy-done.14
  236.6 15.2 %convolution_convert_fusion.1 = bf16[2048,1024]{1,0:T(8,128)(2,1)} fusion(bf16[2048,1024]{1,0:T(8,128)(2,1)} %get-tuple-element.72, f32[2048]{0:T(1024)S(1)} %bitcast.91, f32[2048]{0:T(1024)S(1)} %bitcast.89, f32[2048]{0:T(1024)S(1)} %add_rsqrt_fusion, f32[2048]{0:T(1024)S(1)} %broadcast_multiply_fusion.2, bf16[1024,2048]{1,0:T(8,128)(2,1)} %collective-permute-done, ...), kind=kOutput, calls=%fused_computation.40 | convolution fusion | flops 8629780480 | bytes 16809984 | tf_op jit(solution)/shard_map/dot_general | solution.py:55
  251.9 14.2 %convolution_convert_fusion = bf16[2048,1024]{1,0:T(8,128)(2,1)} fusion(bf16[2048,1024]{1,0:T(8,128)(2,1)} %get-tuple-element.69, bf16[1024,2048]{1,0:T(8,128)(2,1)} %collective-permute-done.2, bf16[1024,2048]{1,0:T(8,128)(2,1)} %bitcast.73), kind=kOutput, calls=%fused_computation.39 | convolution fusion | flops 8608808960 | bytes 16777216 | tf_op jit(solution)/shard_map/dot_general | solution.py:55
  266.2 11.3 %fusion.14 = f32[2048,2048]{1,0:T(8,128)S(1)} fusion(f32[2048,2048]{1,0:T(8,128)} %get-tuple-element.38, f32[2048]{0:T(1024)S(1)} %broadcast_multiply_fusion, f32[2048]{0:T(1024)S(1)} %broadcast_multiply_fusion.1, f32[2048]{0:T(1024)S(1)} %add_rsqrt_fusion, f32[2048]{0:T(1024)S(1)} %broadcast_multiply_fusion.2, bf16[1024,2048]{1,0:T(8,128)(2,1)} %collective-permute-done, ...), kind=kLoop, calls=%fused_computation.16 | loop fusion | flops 41943040 | bytes 41975808 | tf_op jit(solution)/shard_map/mul | solution.py:473
  277.5 5.8 copy-done.3
  283.3 2.7 slice.138
  285.9 7.4 %collective-permute-done.3 = bf16[1024,2048]{1,0:T(8,128)(2,1)S(1)} collective-permute-done((bf16[1024,2048]{1,0:T(8,128)(2,1)}, bf16[1024,2048]{1,0:T(8,128)(2,1)S(1)}, u32[]{:S(2)}, u32[]{:S(2)}) %collective-permute-start.3) | collective-permute-done | bytes 4194336 | tf_op jit(solution)/shard_map/ppermute | solution.py:286
  293.3 7.0 %fusion.23 = bf16[1024,2048]{1,0:T(8,128)(2,1)} fusion(f32[2048,2048]{1,0:T(8,128)} %copy-done.3, bf16[1024,2048]{1,0:T(8,128)(2,1)S(1)} %collective-permute-done.3), kind=kLoop, calls=%fused_computation.31 | loop fusion | flops 6291456 | bytes 16777216 | tf_op jit(solution)/shard_map/convert_element_type | solution.py:414
  300.4 15.6 %fusion.43 = f32[2048,2048]{1,0:T(8,128)} fusion(bf16[2048,1024]{1,0:T(8,128)(2,1)} %get-tuple-element.69, bf16[2048,1024]{1,0:T(8,128)(2,1)} %all-gather.13.cloned.1.call-done), kind=kOutput, calls=%fused_computation.112 | convolution fusion | flops 8589934592 | bytes 25165824 | tf_op jit(solution)/shard_map/dot_general | solution.py:61
  316.0 8.2 %convolution_add_fusion = f32[2048,2048]{1,0:T(8,128)S(1)} fusion(f32[2048,2048]{1,0:T(8,128)} %fusion.43, bf16[2048,256]{1,0:T(8,128)(2,1)S(1)} %copy-done.9, bf16[2048,256]{1,0:T(8,128)(2,1)S(1)} %copy-done.10), kind=kOutput, calls=%fused_computation.23 | convolution fusion | flops 2151677952 | bytes 35651584 | tf_op jit(solution)/shard_map/dot_general | solution.py:61
  324.3 5.8 copy-done.2
  330.0 2.7 slice.139
  332.8 7.2 %collective-permute-done.1 = bf16[1024,2048]{1,0:T(8,128)(2,1)S(1)} collective-permute-done((bf16[1024,2048]{1,0:T(8,128)(2,1)}, bf16[1024,2048]{1,0:T(8,128)(2,1)S(1)}, u32[]{:S(2)}, u32[]{:S(2)}) %collective-permute-start.1) | collective-permute-done | bytes 4194336 | tf_op jit(solution)/shard_map/ppermute | solution.py:286
  340.0 6.9 %fusion.24 = bf16[1024,2048]{1,0:T(8,128)(2,1)} fusion(f32[2048,2048]{1,0:T(8,128)} %copy-done.2, bf16[1024,2048]{1,0:T(8,128)(2,1)S(1)} %collective-permute-done.1), kind=kLoop, calls=%fused_computation.34 | loop fusion | flops 6291456 | bytes 16777216 | tf_op jit(solution)/shard_map/convert_element_type | solution.py:414
  347.0 0.7 add_bitcast_fusion
  348.3 53.5 %all-reduce.3.cloned.1.call-done = f32[24576]{0:T(1024)} async-done(((f32[24576]{0:T(1024)}), f32[24576]{0:T(1024)}) %all-reduce.3.cloned.1.call-update) | async-done | bytes 98320 | tf_op jit(solution)/shard_map/psum | solution.py:492
  401.8 1.4 fusion.37
  403.2 0.8 dynamic_slice.105
  404.0 0.6 broadcast_in_dim.66
  404.7 1.0 convert_dynamic-update-slice_fusion.7
  405.8 52.5 %reduce-scatter.15.cloned.1.call-done = bf16[512,1024]{1,0:T(8,128)(2,1)} async-done(((bf16[2048,1024]{1,0:T(8,128)(2,1)}), bf16[512,1024]{1,0:T(8,128)(2,1)}) %reduce-scatter.15.cloned.1.call-update) | async-done | bytes 1048592 | tf_op jit(solution)/shard_map/reduce_scatter | solution.py:424
  458.3 2.0 broadcast_in_dim.65
  460.4 2.4 convert_dynamic-update-slice_fusion.5
  462.8 51.2 %reduce-scatter.17.cloned.1.call-done = bf16[512,1024]{1,0:T(8,128)(2,1)} async-done(((bf16[2048,1024]{1,0:T(8,128)(2,1)}), bf16[512,1024]{1,0:T(8,128)(2,1)}) %reduce-scatter.17.cloned.1.call-update) | async-done | bytes 1048592 | tf_op jit(solution)/shard_map/reduce_scatter | solution.py:424
  513.9 1.3 convert_dynamic-update-slice_fusion.4
  515.2 2.5 broadcast.62.clone
  517.7 1.6 convert_dynamic-update-slice_fusion.3
  519.3 2.5 broadcast.62.clone.1
  521.8 1.6 convert_dynamic-update-slice_fusion.1
  523.4 2.8 convert_dynamic-update-slice_fusion.2
  526.2 1.6 convert_dynamic-update-slice_fusion
  527.7 65.2 %reduce-scatter.9.cloned.1.call-done = bf16[1024,512]{1,0:T(8,128)(2,1)} async-done(((bf16[1024,2048]{1,0:T(8,128)(2,1)}), bf16[1024,512]{1,0:T(8,128)(2,1)}) %reduce-scatter.9.cloned.1.call-update) | async-done | bytes 1048592 | tf_op jit(solution)/shard_map/reduce_scatter | solution.py:413
  592.9 3.2 convert_add_fusion
  596.1 76.5 %reduce-scatter.7.cloned.1.call-done = bf16[1024,512]{1,0:T(8,128)(2,1)} async-done(((bf16[1024,2048]{1,0:T(8,128)(2,1)}), bf16[1024,512]{1,0:T(8,128)(2,1)}) %reduce-scatter.7.cloned.1.call-update) | async-done | bytes 1048592 | tf_op jit(solution)/shard_map/reduce_scatter | solution.py:413
  672.5 3.2 add_add_fusion
  (158 shorter events, 6.1 us)
Async XLA Ops:
  7.2 4.2 copy-start
  7.2 8.3 %copy-start.19 = (s32[4]{0:T(128)S(1)}, s32[4]{0:T(128)}, u32[]{:S(2)}) copy-start(s32[4]{0:T(128)} %param.19) | copy-start | bytes 52
  7.2 11.6 %copy-start.17 = (s32[1,2048]{1,0:T(1,128)S(1)}, s32[1,2048]{1,0:T(1,128)}, u32[]{:S(2)}) copy-start(s32[1,2048]{1,0:T(1,128)} %param.18) | copy-start | bytes 24580
  7.2 13.8 %copy-start.21 = (bf16[1,384]{1,0:T(2,128)(2,1)S(1)}, bf16[1,384]{1,0:T(2,128)(2,1)}, u32[]{:S(2)}) copy-start(bf16[1,384]{1,0:T(2,128)(2,1)} %param.23) | copy-start | bytes 2308
  7.2 13.8 %copy-start.20 = (bf16[1,512]{1,0:T(2,128)(2,1)S(1)}, bf16[1,512]{1,0:T(2,128)(2,1)}, u32[]{:S(2)}) copy-start(bf16[1,512]{1,0:T(2,128)(2,1)} %param.29) | copy-start | bytes 3076
  7.2 13.9 %copy-start.22 = (bf16[512]{0:T(512)(128)(2,1)S(1)}, bf16[512]{0:T(512)(128)(2,1)}, u32[]{:S(2)}) copy-start(bf16[512]{0:T(512)(128)(2,1)} %param.20) | copy-start | bytes 3076
  7.2 14.1 %copy-start.23 = (bf16[512]{0:T(512)(128)(2,1)S(1)}, bf16[512]{0:T(512)(128)(2,1)}, u32[]{:S(2)}) copy-start(bf16[512]{0:T(512)(128)(2,1)} %param.21) | copy-start | bytes 3076
  7.3 14.3 %copy-start.24 = (bf16[512]{0:T(512)(128)(2,1)S(1)}, bf16[512]{0:T(512)(128)(2,1)}, u32[]{:S(2)}) copy-start(bf16[512]{0:T(512)(128)(2,1)} %param.26) | copy-start | bytes 3076
  7.3 14.5 %copy-start.25 = (bf16[512]{0:T(512)(128)(2,1)S(1)}, bf16[512]{0:T(512)(128)(2,1)}, u32[]{:S(2)}) copy-start(bf16[512]{0:T(512)(128)(2,1)} %param.27) | copy-start | bytes 3076
  7.3 14.7 %copy-start.26 = (bf16[512]{0:T(512)(128)(2,1)S(1)}, bf16[512]{0:T(512)(128)(2,1)}, u32[]{:S(2)}) copy-start(bf16[512]{0:T(512)(128)(2,1)} %param.25) | copy-start | bytes 3076
  7.3 15.0 %copy-start.27 = (bf16[512]{0:T(512)(128)(2,1)S(1)}, bf16[512]{0:T(512)(128)(2,1)}, u32[]{:S(2)}) copy-start(bf16[512]{0:T(512)(128)(2,1)} %param.31) | copy-start | bytes 3076
  7.3 49.2 %all-gather.9.cloned.1.call-start = ((), (), s32[]{:S(2)}) async-start(), calls=%async_computation.7 | async-start | bytes 1310720 | tf_op jit(solution)/shard_map/all_gather | solution.py:323
  9.2 76.5 %all-gather.7.cloned.1.call-start = ((), (), s32[]{:S(2)}) async-start(), calls=%async_computation.6 | async-start | bytes 3932160 | tf_op jit(solution)/shard_map/all_gather | solution.py:323
  11.3 157.3 %all-gather.11.cloned.1.call-start = ((), (), s32[]{:S(2)}) async-start(), calls=%async_computation.8 | async-start | bytes 5242880 | tf_op jit(solution)/shard_map/all_gather | solution.py:323
  12.5 183.1 %all-gather.13.cloned.1.call-start = ((), (), s32[]{:S(2)}) async-start(), calls=%async_computation.9 | async-start | bytes 5242880 | tf_op jit(solution)/shard_map/all_gather | solution.py:323
  12.5 29.5 %collective-permute-start = (bf16[1024,2048]{1,0:T(8,128)(2,1)}, bf16[1024,2048]{1,0:T(8,128)(2,1)}, u32[]{:S(2)}, u32[]{:S(2)}) collective-permute-start(bf16[1024,2048]{1,0:T(8,128)(2,1)} %bitcast.60), channel_id=1, source_target_pairs={{0,4},{4,0},{1,5},{5,1},{2,6},{6,2},{3,7},{7,3},{8,12},{12,8},{9,1... | collective-permute-start | bytes 12582920 | tf_op jit(solution)/shard_map/ppermute | solution.py:286
  13.1 40.0 %collective-permute-start.2 = (bf16[1024,2048]{1,0:T(8,128)(2,1)}, bf16[1024,2048]{1,0:T(8,128)(2,1)}, u32[]{:S(2)}, u32[]{:S(2)}) collective-permute-start(bf16[1024,2048]{1,0:T(8,128)(2,1)} %bitcast.70), channel_id=1, source_target_pairs={{0,4},{4,0},{1,5},{5,1},{2,6},{6,2},{3,7},{7,3},{8,12},{12,8},{9,1... | collective-permute-start | bytes 12582920 | tf_op jit(solution)/shard_map/ppermute | solution.py:286
  15.5 332.3 %reduce-scatter.13.cloned.1.call-start = ((), (), s32[]{:S(2)}) async-start(), calls=%async_computation.14 | async-start | bytes 1310720 | tf_op jit(solution)/shard_map/reduce_scatter | solution.py:424
  18.9 27.8 %copy-start.15 = (s32[2048]{0:T(1024)}, s32[2048]{0:T(1024)S(1)}, u32[]{:S(2)}) copy-start(s32[2048]{0:T(1024)S(1)} %pad_add_fusion) | copy-start | bytes 24580
  32.6 0.6 copy-start.16
  38.0 8.8 %copy-start.4 = (bf16[1,2,512,2048]{3,2,1,0:T(8,128)(2,1)S(1)}, bf16[1,2,512,2048]{3,2,1,0:T(8,128)(2,1)}, u32[]{:S(2)}) copy-start(bf16[1,2,512,2048]{3,2,1,0:T(8,128)(2,1)} %param.16) | copy-start | bytes 12582916
  42.0 11.1 %copy-start.7 = (bf16[1,2,512,2048]{3,2,1,0:T(8,128)(2,1)S(1)}, bf16[1,2,512,2048]{3,2,1,0:T(8,128)(2,1)}, u32[]{:S(2)}) copy-start(bf16[1,2,512,2048]{3,2,1,0:T(8,128)(2,1)} %param.17) | copy-start | bytes 12582916
  100.8 18.1 %copy-start.8 = (bf16[1,2,512,2048]{3,2,1,0:T(8,128)(2,1)S(1)}, bf16[1,2,512,2048]{3,2,1,0:T(8,128)(2,1)}, u32[]{:S(2)}) copy-start(bf16[1,2,512,2048]{3,2,1,0:T(8,128)(2,1)} %param.17) | copy-start | bytes 12582916
  125.0 223.0 %reduce-scatter.11.cloned.1.call-start = ((), (), s32[]{:S(2)}) async-start(), calls=%async_computation.13 | async-start | bytes 3932160 | tf_op jit(solution)/shard_map/reduce_scatter | solution.py:424
  125.0 17.5 %copy-start.5 = (bf16[1,2,512,2048]{3,2,1,0:T(8,128)(2,1)S(1)}, bf16[1,2,512,2048]{3,2,1,0:T(8,128)(2,1)}, u32[]{:S(2)}) copy-start(bf16[1,2,512,2048]{3,2,1,0:T(8,128)(2,1)} %param.16) | copy-start | bytes 12582916
  142.6 12.8 %copy-start.18 = (f32[1,768]{1,0:T(1,128)S(1)}, f32[1,768]{1,0:T(1,128)}, u32[]{:S(2)}) copy-start(f32[1,768]{1,0:T(1,128)} %get-tuple-element.26) | copy-start | bytes 9220
  155.3 246.5 %all-reduce.3.cloned.1.call-start = ((), (), s32[]{:S(2)}) async-start(), calls=%async_computation.12 | async-start | bytes 196608 | tf_op jit(solution)/shard_map/psum | solution.py:492
  195.6 17.5 %copy-start.6 = (bf16[1,2,512,2048]{3,2,1,0:T(8,128)(2,1)S(1)}, bf16[1,2,512,2048]{3,2,1,0:T(8,128)(2,1)}, u32[]{:S(2)}) copy-start(bf16[1,2,512,2048]{3,2,1,0:T(8,128)(2,1)} %param.16) | copy-start | bytes 12582916
  195.6 17.5 %copy-start.28 = (bf16[2048,1024]{1,0:T(8,128)(2,1)S(1)}, bf16[2048,1024]{1,0:T(8,128)(2,1)}, u32[]{:S(2)}) copy-start(bf16[2048,1024]{1,0:T(8,128)(2,1)} %all-gather.11.cloned.1.call-done) | copy-start | bytes 12582916
  235.9 0.6 copy-start.14
  236.5 221.8 %reduce-scatter.15.cloned.1.call-start = ((), (), s32[]{:S(2)}) async-start(), calls=%async_computation.15 | async-start | bytes 5242880 | tf_op jit(solution)/shard_map/reduce_scatter | solution.py:424
  251.8 262.1 %reduce-scatter.17.cloned.1.call-start = ((), (), s32[]{:S(2)}) async-start(), calls=%async_computation.16 | async-start | bytes 5242880 | tf_op jit(solution)/shard_map/reduce_scatter | solution.py:424
  266.2 326.7 %reduce-scatter.9.cloned.1.call-start = ((), (), s32[]{:S(2)}) async-start(), calls=%async_computation.11 | async-start | bytes 5242880 | tf_op jit(solution)/shard_map/reduce_scatter | solution.py:413
  277.5 5.8 copy-start.3
  285.9 7.4 %collective-permute-start.3 = (bf16[1024,2048]{1,0:T(8,128)(2,1)}, bf16[1024,2048]{1,0:T(8,128)(2,1)S(1)}, u32[]{:S(2)}, u32[]{:S(2)}) collective-permute-start(bf16[1024,2048]{1,0:T(8,128)(2,1)} %slice.138), channel_id=1, source_target_pairs={{0,4},{4,0},{1,5},{5,1},{2,6},{6,2},{3,7},{7,3},{8,12},{12,8},{9,1... | collective-permute-start | bytes 12582920 | tf_op jit(solution)/shard_map/ppermute | solution.py:286
  300.3 15.7 %copy-start.9 = (bf16[2048,256]{1,0:T(8,128)(2,1)S(1)}, bf16[2048,256]{1,0:T(8,128)(2,1)}, u32[]{:S(2)}) copy-start(bf16[2048,256]{1,0:T(8,128)(2,1)} %get-tuple-element.20.attn_ref) | copy-start | bytes 3145732
  300.3 15.7 %copy-start.10 = (bf16[2048,256]{1,0:T(8,128)(2,1)S(1)}, bf16[2048,256]{1,0:T(8,128)(2,1)}, u32[]{:S(2)}) copy-start(bf16[2048,256]{1,0:T(8,128)(2,1)} %all-gather.9.cloned.1.call-done) | copy-start | bytes 3145732
  300.3 372.2 %reduce-scatter.7.cloned.1.call-start = ((), (), s32[]{:S(2)}) async-start(), calls=%async_computation.10 | async-start | bytes 5242880 | tf_op jit(solution)/shard_map/reduce_scatter | solution.py:413
  324.2 5.8 copy-start.2
  332.7 7.4 %collective-permute-start.1 = (bf16[1024,2048]{1,0:T(8,128)(2,1)}, bf16[1024,2048]{1,0:T(8,128)(2,1)S(1)}, u32[]{:S(2)}, u32[]{:S(2)}) collective-permute-start(bf16[1024,2048]{1,0:T(8,128)(2,1)} %slice.139), channel_id=1, source_target_pairs={{0,4},{4,0},{1,5},{5,1},{2,6},{6,2},{3,7},{7,3},{8,12},{12,8},{9,1... | collective-permute-start | bytes 12582920 | tf_op jit(solution)/shard_map/ppermute | solution.py:286
  347.8 57.9 %collective-permute-start.5 = (bf16[512,256]{1,0:T(8,128)(2,1)}, bf16[512,256]{1,0:T(8,128)(2,1)S(1)}, u32[]{:S(2)}, u32[]{:S(2)}) collective-permute-start(bf16[512,256]{1,0:T(8,128)(2,1)} %reduce-scatter.13.cloned.1.call-done), channel_id=1, source_target_pairs={{0,4},{4,0},{1,5},{5,1},{2,6},{6,2},{3,7},{7,3},{8,12},{12,8},{9,1... | collective-permute-start | bytes 786440 | tf_op jit(solution)/shard_map/ppermute | solution.py:286
  348.0 166.0 %collective-permute-start.4 = (bf16[512,768]{1,0:T(8,128)(2,1)}, bf16[512,768]{1,0:T(8,128)(2,1)S(1)}, u32[]{:S(2)}, u32[]{:S(2)}) collective-permute-start(bf16[512,768]{1,0:T(8,128)(2,1)} %reduce-scatter.11.cloned.1.call-done), channel_id=1, source_target_pairs={{0,4},{4,0},{1,5},{5,1},{2,6},{6,2},{3,7},{7,3},{8,12},{12,8},{9,1... | collective-permute-start | bytes 2359304 | tf_op jit(solution)/shard_map/ppermute | solution.py:286
  405.8 57.0 %copy-start.13 = (f32[512,512]{1,0:T(8,128)}, f32[512,512]{1,0:T(8,128)S(1)}, u32[]{:S(2)}) copy-start(f32[512,512]{1,0:T(8,128)S(1)} %convert_dynamic-update-slice_fusion.6) | copy-start | bytes 3145732
  458.3 59.4 %copy-start.11 = (bf16[512,1024]{1,0:T(8,128)(2,1)S(1)}, bf16[512,1024]{1,0:T(8,128)(2,1)}, u32[]{:S(2)}) copy-start(bf16[512,1024]{1,0:T(8,128)(2,1)} %reduce-scatter.15.cloned.1.call-done) | copy-start | bytes 3145732
  458.3 65.1 %collective-permute-start.6 = (bf16[512,1024]{1,0:T(8,128)(2,1)}, bf16[512,1024]{1,0:T(8,128)(2,1)}, u32[]{:S(2)}, u32[]{:S(2)}) collective-permute-start(bf16[512,1024]{1,0:T(8,128)(2,1)} %reduce-scatter.15.cloned.1.call-done), channel_id=1, source_target_pairs={{0,4},{4,0},{1,5},{5,1},{2,6},{6,2},{3,7},{7,3},{8,12},{12,8},{9,1... | collective-permute-start | bytes 3145736 | tf_op jit(solution)/shard_map/ppermute | solution.py:286
  513.9 7.9 %copy-start.12 = (bf16[512,1024]{1,0:T(8,128)(2,1)S(1)}, bf16[512,1024]{1,0:T(8,128)(2,1)}, u32[]{:S(2)}) copy-start(bf16[512,1024]{1,0:T(8,128)(2,1)} %reduce-scatter.17.cloned.1.call-done) | copy-start | bytes 3145732
  513.9 12.2 %collective-permute-start.7 = (bf16[512,1024]{1,0:T(8,128)(2,1)}, bf16[512,1024]{1,0:T(8,128)(2,1)S(1)}, u32[]{:S(2)}, u32[]{:S(2)}) collective-permute-start(bf16[512,1024]{1,0:T(8,128)(2,1)} %reduce-scatter.17.cloned.1.call-done), channel_id=1, source_target_pairs={{0,4},{4,0},{1,5},{5,1},{2,6},{6,2},{3,7},{7,3},{8,12},{12,8},{9,1... | collective-permute-start | bytes 3145736 | tf_op jit(solution)/shard_map/ppermute | solution.py:286
  519.3 156.5 %copy-start.1 = (bf16[512,2048]{1,0:T(8,128)(2,1)S(1)}, bf16[512,2048]{1,0:T(8,128)(2,1)}, u32[]{:S(2)}) copy-start(bf16[512,2048]{1,0:T(8,128)(2,1)} %param.28) | copy-start | bytes 6291460
Sparse Core Ops, SparseCore 0:
  10.0 29.2 all-gather.8
  41.6 43.9 all-gather.6
  88.1 52.5 all-gather.10
  143.0 52.5 all-gather.12
  198.3 27.9 reduce-scatter.12
  229.1 43.8 reduce-scatter.10
  279.2 122.5 all-reduce.2
  404.8 53.4 reduce-scatter.14
  461.3 52.5 reduce-scatter.16
  516.1 76.7 reduce-scatter.8
  595.2 77.2 reduce-scatter.6
